TPU v7x, 8 devices: a whole 2x2x1 slice. The times are simulated.
8 devices in a mesh: model: 2 (over z, y), data: 4 (over x, core).
Axes of the slice: x: 2, y: 2, z: 1, core: 2. Of those that a mesh axis runs over, the one named last changes fastest.
Arguments:
- grad_qkv: float32 [4, 4, 768, 2304], P('data', None, None, 'model')
- weight_qkv: float32 [4, 768, 2304], P(None, 'data', 'model')
- moment1_qkv: float32 [4, 768, 2304], P(None, 'data', 'model')
- moment2_qkv: float32 [4, 768, 2304], P(None, 'data', 'model')
- grad_proj: float32 [4, 4, 768, 768], P('data', None, 'model')
- weight_proj: float32 [4, 768, 768], P(None, ('model', 'data'))
- moment1_proj: float32 [4, 768, 768], P(None, ('model', 'data'))
- moment2_proj: float32 [4, 768, 768], P(None, ('model', 'data'))
- grad_fcin: float32 [4, 4, 768, 3072], P('data', None, None, 'model')
- weight_fcin: float32 [4, 768, 3072], P(None, 'data', 'model')
- moment1_fcin: float32 [4, 768, 3072], P(None, 'data', 'model')
- moment2_fcin: float32 [4, 768, 3072], P(None, 'data', 'model')
- grad_fcout: float32 [4, 4, 3072, 768], P('data', None, 'model')
- weight_fcout: float32 [4, 3072, 768], P(None, ('model', 'data'))
- moment1_fcout: float32 [4, 3072, 768], P(None, ('model', 'data'))
- moment2_fcout: float32 [4, 3072, 768], P(None, ('model', 'data'))
Outputs:
- output 1: bfloat16 [4, 768, 2304], P(None, None, 'model')
- output 2: bfloat16 [4, 768, 768], P(None, 'model')
- output 3: bfloat16 [4, 768, 3072], P(None, None, 'model')
- output 4: bfloat16 [4, 3072, 768], P(None, 'model')
- output 5: float32 [4, 768, 2304], P(None, 'data', 'model')
- output 6: float32 [4, 768, 768], P(None, ('model', 'data'))
- output 7: float32 [4, 768, 3072], P(None, 'data', 'model')
- output 8: float32 [4, 3072, 768], P(None, ('model', 'data'))
- output 9: float32 [4, 768, 2304], P(None, 'data', 'model')
- output 10: float32 [4, 768, 768], P(None, ('model', 'data'))
- output 11: float32 [4, 768, 3072], P(None, 'data', 'model')
- output 12: float32 [4, 3072, 768], P(None, ('model', 'data'))
- output 13: float32 [4, 768, 2304], P(None, 'data', 'model')
- output 14: float32 [4, 768, 768], P(None, ('model', 'data'))
- output 15: float32 [4, 768, 3072], P(None, 'data', 'model')
- output 16: float32 [4, 3072, 768], P(None, ('model', 'data'))
All inputs are finite; a program needn't handle non-finite values.
Results may differ from a plain program's by a relative error of at most 0.001.
Values are sent between devices in bfloat16 or wider.
A program may use at most 1 GiB of HBM per device.

v0:
```python
import jax
import jax.numpy as jnp
from jax import lax
from jax.sharding import PartitionSpec as P

LEARN_RATE = 0.08
BETA_ONE = 0.9
BETA_TWO = 0.999
ADAM_EPS = 1e-6
DECAY_RATE = 0.01
MAX_NORM = 1.0
STEP_COUNT = 100
COLUMN_SPLIT = (True, False, True, False)


def grad_spec(col_split):
    return P("data", None, None, "model") if col_split else P("data", None, "model", None)


def state_spec(col_split):
    return P(None, "data", "model") if col_split else P(None, ("model", "data"), None)


def replica_spec(col_split):
    return P(None, None, "model") if col_split else P(None, "model", None)


def adam_direction(grad_mean, weight, moment1, moment2, clip_coef):
    clipped = clip_coef * grad_mean
    new_first = BETA_ONE * moment1 + (1.0 - BETA_ONE) * clipped
    new_second = BETA_TWO * moment2 + (1.0 - BETA_TWO) * clipped * clipped
    first_hat = new_first / (1.0 - BETA_ONE ** STEP_COUNT)
    second_hat = new_second / (1.0 - BETA_TWO ** STEP_COUNT)
    update = first_hat / (jnp.sqrt(second_hat) + ADAM_EPS) + DECAY_RATE * weight
    return update, new_first, new_second


def solution(mesh):
    group_size = mesh.shape["data"]
    in_specs = []
    for col_split in COLUMN_SPLIT:
        in_specs.extend([grad_spec(col_split), state_spec(col_split), state_spec(col_split), state_spec(col_split)])
    out_specs = tuple([replica_spec(col_split) for col_split in COLUMN_SPLIT] + [state_spec(col_split) for col_split in COLUMN_SPLIT] * 3)

    def device_step(*arrays):
        kind_count = len(COLUMN_SPLIT)
        grad_means = []
        for kind_idx in range(kind_count):
            sent_grad = arrays[4 * kind_idx].astype(jnp.bfloat16)
            received = lax.all_to_all(sent_grad, "data", 2, 0, tiled=True)
            grad_means.append(jnp.sum(received, axis=0, dtype=jnp.float32) / group_size)
        local_sq = sum(jnp.sum(grad_mean * grad_mean) for grad_mean in grad_means)
        total_norm = jnp.sqrt(lax.psum(local_sq, ("model", "data")))
        clip_coef = jnp.minimum(1.0, MAX_NORM / total_norm)
        replicas, weights, firsts, seconds = [], [], [], []
        for kind_idx in range(kind_count):
            weight = arrays[4 * kind_idx + 1]
            update, new_first, new_second = adam_direction(grad_means[kind_idx], weight, arrays[4 * kind_idx + 2], arrays[4 * kind_idx + 3], clip_coef)
            sq_pair = jnp.stack([jnp.sum(weight * weight, axis=(1, 2)), jnp.sum(update * update, axis=(1, 2))])
            norm_pair = jnp.sqrt(lax.psum(sq_pair, ("model", "data")))
            trust_ratio = (norm_pair[0] / norm_pair[1])[:, None, None]
            new_weight = weight - LEARN_RATE * trust_ratio * update
            replicas.append(lax.all_gather(new_weight.astype(jnp.bfloat16), "data", axis=1, tiled=True))
            weights.append(new_weight)
            firsts.append(new_first)
            seconds.append(new_second)
        return tuple(replicas + weights + firsts + seconds)

    return jax.shard_map(device_step, mesh=mesh, in_specs=tuple(in_specs), out_specs=out_specs, check_vma=False)
```

profile of v0, /device:TPU:0, one launch (start us, length us, event | category | flops | bytes accessed | tf_op | source)
XLA Modules:
  0.0 669.7 jit_solution(457746771986029317)
XLA Ops:
  7.2 6.8 %copy.151 = bf16[1,4,384,768]{3,1,0,2:T(4,128)(2,1)} copy(f32[1,4,384,768]{3,2,1,0:T(8,128)} %param.20) | data formatting | bytes 7077888 | tf_op args[4]
  14.0 4.6 all-to-all-start.1
  18.6 14.8 %copy.150 = bf16[1,4,768,1152]{3,1,0,2:T(4,128)(2,1)} copy(f32[1,4,768,1152]{3,2,1,0:T(8,128)} %param.16) | data formatting | bytes 21233664 | tf_op args[0]
  33.3 13.5 %all-to-all-done.1 = bf16[1,4,384,768]{3,1,0,2:T(4,128)(2,1)S(1)} async-done(((bf16[1,4,384,768]{3,1,0,2:T(4,128)(2,1)}), bf16[1,4,384,768]{3,1,0,2:T(4,128)(2,1)S(1)}, u32[]{:S(2)}, u32[]{:S(2)}) %all-to-all-start.1) | async-done | bytes 2359328 | tf_op jit(solution)/shard_map/all_to_all | solution.py:50
  46.9 5.4 all-to-all-start
  52.3 22.3 %copy.149 = bf16[1,4,768,1536]{3,1,0,2:T(4,128)(2,1)} copy(f32[1,4,768,1536]{3,2,1,0:T(8,128)} %param.24) | data formatting | bytes 28311552 | tf_op args[8]
  74.6 56.5 %all-to-all-done = bf16[1,4,768,1152]{3,1,0,2:T(4,128)(2,1)} async-done(((bf16[1,4,768,1152]{3,1,0,2:T(4,128)(2,1)}), bf16[1,4,768,1152]{3,1,0,2:T(4,128)(2,1)}, u32[]{:S(2)}, u32[]{:S(2)}) %all-to-all-start) | async-done | bytes 7077920 | tf_op jit(solution)/shard_map/all_to_all | solution.py:50
  131.1 5.8 all-to-all-start.2
  136.9 22.3 %copy.148 = bf16[1,4,1536,768]{3,1,0,2:T(4,128)(2,1)} copy(f32[1,4,1536,768]{3,2,1,0:T(8,128)} %param.28) | data formatting | bytes 28311552 | tf_op args[12]
  159.2 81.7 %all-to-all-done.2 = bf16[1,4,768,1536]{3,1,0,2:T(4,128)(2,1)} async-done(((bf16[1,4,768,1536]{3,1,0,2:T(4,128)(2,1)}), bf16[1,4,768,1536]{3,1,0,2:T(4,128)(2,1)}, u32[]{:S(2)}, u32[]{:S(2)}) %all-to-all-start.2) | async-done | bytes 9437216 | tf_op jit(solution)/shard_map/all_to_all | solution.py:50
  240.9 5.8 all-to-all-start.3
  249.3 7.3 %convert_reduce_fusion.2 = f32[4,192,1152]{2,0,1:T(4,128)S(1)} fusion(bf16[4,4,192,1152]{3,0,2,1:T(4,128)(2,1)} %bitcast.16), kind=kLoop, calls=%fused_computation.4 | loop fusion | flops 6193152 | bytes 10616832 | tf_op jit(solution)/shard_map/reduce_sum | solution.py:51
  260.3 10.6 %convert_reduce_fusion.1 = f32[4,192,1536]{2,0,1:T(4,128)S(1)} fusion(bf16[4,4,192,1536]{3,0,2,1:T(4,128)(2,1)} %bitcast.18), kind=kLoop, calls=%fused_computation.1 | loop fusion | flops 8257536 | bytes 14155776 | tf_op jit(solution)/shard_map/reduce_sum | solution.py:51
  276.1 74.6 %all-to-all-done.3 = bf16[1,4,1536,768]{3,1,0,2:T(4,128)(2,1)} async-done(((bf16[1,4,1536,768]{3,1,0,2:T(4,128)(2,1)}), bf16[1,4,1536,768]{3,1,0,2:T(4,128)(2,1)}, u32[]{:S(2)}, u32[]{:S(2)}) %all-to-all-start.3) | async-done | bytes 9437216 | tf_op jit(solution)/shard_map/all_to_all | solution.py:50
  350.8 10.0 %convert_reduce_fusion = f32[4,384,768]{2,0,1:T(4,128)S(1)} fusion(bf16[4,4,384,768]{3,0,2,1:T(4,128)(2,1)} %bitcast.19), kind=kLoop, calls=%fused_computation | loop fusion | flops 8257536 | bytes 14155776 | tf_op jit(solution)/shard_map/reduce_sum | solution.py:51
  367.3 23.1 %psum.35 = f32[]{:T(128)} all-reduce(f32[]{:T(128)S(6)} %add.81), channel_id=1, replica_groups=mesh['model'=2,'data'=4] {'model','data'}, use_global_device_ids=true, to_apply=%region_9.0 | all-reduce | flops 1 | bytes 8 | tf_op jit(solution)/shard_map/psum | solution.py:53
  391.2 11.9 %multiply_reduce_fusion.1 = (f32[4]{0:T(128)S(1)}, f32[4]{0:T(128)S(1)}, f32[4,384,768]{2,1,0:T(8,128)}, f32[4,384,768]{2,1,0:T(8,128)}) fusion(f32[4,384,768]{2,1,0:T(8,128)} %param.29, f32[]{:T(128)S(6)} %mul.277, f32[4,384,768]{2,0,1:T(4,128)} %copy-done.1, f32[4,384,768]{2,1,0:T(8,128)} %param.30, f32[4,384,768]{2,1,0:T(8,128)} %param.31), kind=kLoop, calls=%fused_computation.19 | loop fusion | flops 21233656 | bytes 28311588 | tf_op jit(solution)/shard_map/reduce_sum | solution.py:59
  403.1 12.0 %multiply_reduce_fusion.3 = (f32[4]{0:T(128)S(1)}, f32[4]{0:T(128)S(1)}, f32[4,192,1536]{2,1,0:T(8,128)}, f32[4,192,1536]{2,1,0:T(8,128)}) fusion(f32[4,192,1536]{2,1,0:T(8,128)} %param.25, f32[]{:T(128)S(6)} %mul.277, f32[4,192,1536]{2,0,1:T(4,128)S(1)} %bitcast.25, f32[4,192,1536]{2,1,0:T(8,128)} %param.26, f32[4,192,1536]{2,1,0:T(8,128)} %param.27), kind=kLoop, calls=%fused_computation.24 | loop fusion | flops 21233656 | bytes 28311588 | tf_op jit(solution)/shard_map/reduce_sum | solution.py:59
  415.1 5.8 multiply_reduce_fusion.8
  423.4 24.4 %all-reduce = (f32[2,4]{1,0:T(2,128)}, f32[2,4]{1,0:T(2,128)}, f32[2,4]{1,0:T(2,128)}, f32[2,4]{1,0:T(2,128)}) all-reduce(f32[2,4]{1,0:T(2,128)S(1)} %get-tuple-element.92, f32[2,4]{1,0:T(2,128)S(1)} %get-tuple-element.93, f32[2,4]{1,0:T(2,128)S(1)} %get-tuple-element.94, ...), channel_id=1, replica_groups=mesh['model'=2,'data'=4] {'model','data'}, use_global_device_ids=true, to_apply=%region_11.0 | all-reduce | flops 32 | bytes 256 | tf_op jit(solution)/shard_map/psum | solution.py:60
  448.5 3.7 fusion.6
  453.7 6.8 %fusion.7 = (bf16[4,192,1152]{2,1,0:T(8,128)(2,1)S(1)}, f32[4,192,1152]{2,1,0:T(8,128)}) fusion(f32[4,192,1152]{2,1,0:T(8,128)S(1)} %copy-done.5, f32[4,192,1152]{2,1,0:T(8,128)} %get-tuple-element.91, f32[4,192,1152]{2,1,0:T(8,128)} %get-tuple-element.90, f32[4]{0:T(128)S(1)} %multiply_bitcast_fusion.3), kind=kLoop, calls=%fused_computation.59 | loop fusion | flops 7962624 | bytes 15925264 | tf_op jit(solution)/shard_map/convert_element_type | solution.py:63
  463.2 7.8 %fusion.4 = (bf16[4,384,768]{2,1,0:T(8,128)(2,1)S(1)}, f32[4,384,768]{2,1,0:T(8,128)}) fusion(f32[4,384,768]{2,1,0:T(8,128)} %param.29, f32[4,384,768]{2,1,0:T(8,128)} %get-tuple-element.85, f32[4,384,768]{2,1,0:T(8,128)} %get-tuple-element.84, f32[4]{0:T(128)S(1)} %multiply_bitcast_fusion), kind=kLoop, calls=%fused_computation.56 | loop fusion | flops 10616832 | bytes 21233680 | tf_op jit(solution)/shard_map/convert_element_type | solution.py:63
  471.0 3.2 copy.119
  474.6 7.8 %fusion.5 = (bf16[4,192,1536]{2,1,0:T(8,128)(2,1)S(1)}, f32[4,192,1536]{2,1,0:T(8,128)}) fusion(f32[4,192,1536]{2,1,0:T(8,128)} %param.25, f32[4,192,1536]{2,1,0:T(8,128)} %get-tuple-element.87, f32[4,192,1536]{2,1,0:T(8,128)} %get-tuple-element.86, f32[4]{0:T(128)S(1)} %multiply_bitcast_fusion.1), kind=kLoop, calls=%fused_computation.57 | loop fusion | flops 10616832 | bytes 21233680 | tf_op jit(solution)/shard_map/convert_element_type | solution.py:63
  485.7 3.4 copy.121
  489.1 36.7 %all-gather.5.cloned.1.call-done = bf16[4,768,1152]{2,0,1:T(4,128)(2,1)} async-done(((bf16[4,192,1152]{2,0,1:T(4,128)(2,1)}), bf16[4,768,1152]{2,0,1:T(4,128)(2,1)}) %all-gather.5.cloned.1.call-update) | async-done | bytes 7077904 | tf_op jit(solution)/shard_map/all_gather | solution.py:63
  525.8 6.9 %copy.120 = bf16[4,768,1152]{2,1,0:T(8,128)(2,1)} copy(bf16[4,768,1152]{2,0,1:T(4,128)(2,1)} %all-gather.5.cloned.1.call-done) | data formatting | bytes 14155776
  532.6 57.1 %all-gather.11.cloned.1.call-done = bf16[4,1536,768]{2,0,1:T(4,128)(2,1)} async-done(((bf16[4,384,768]{2,0,1:T(4,128)(2,1)}), bf16[4,1536,768]{2,0,1:T(4,128)(2,1)}) %all-gather.11.cloned.1.call-update) | async-done | bytes 9437200 | tf_op jit(solution)/shard_map/all_gather | solution.py:63
  589.7 8.6 %copy.123 = bf16[4,1536,768]{2,1,0:T(8,128)(2,1)} copy(bf16[4,1536,768]{2,0,1:T(4,128)(2,1)} %all-gather.11.cloned.1.call-done) | data formatting | bytes 18874368
  598.3 55.1 %all-gather.9.cloned.1.call-done = bf16[4,768,1536]{2,0,1:T(4,128)(2,1)} async-done(((bf16[4,192,1536]{2,0,1:T(4,128)(2,1)}), bf16[4,768,1536]{2,0,1:T(4,128)(2,1)}) %all-gather.9.cloned.1.call-update) | async-done | bytes 9437200 | tf_op jit(solution)/shard_map/all_gather | solution.py:63
  653.5 9.3 %copy.122 = bf16[4,768,1536]{2,1,0:T(8,128)(2,1)} copy(bf16[4,768,1536]{2,0,1:T(4,128)(2,1)} %all-gather.9.cloned.1.call-done) | data formatting | bytes 18874368
  (65 shorter events, 26.5 us)
Async XLA Ops:
  14.0 32.9 %all-to-all-start.1 = ((bf16[1,4,384,768]{3,1,0,2:T(4,128)(2,1)}), bf16[1,4,384,768]{3,1,0,2:T(4,128)(2,1)S(1)}, u32[]{:S(2)}, u32[]{:S(2)}) async-start(bf16[1,4,384,768]{3,1,0,2:T(4,128)(2,1)} %copy.151), calls=%async_computation.1 | async-start | bytes 4718592 | tf_op jit(solution)/shard_map/all_to_all | solution.py:50
  46.9 84.2 %all-to-all-start = ((bf16[1,4,768,1152]{3,1,0,2:T(4,128)(2,1)}), bf16[1,4,768,1152]{3,1,0,2:T(4,128)(2,1)}, u32[]{:S(2)}, u32[]{:S(2)}) async-start(bf16[1,4,768,1152]{3,1,0,2:T(4,128)(2,1)} %copy.150), calls=%async_computation | async-start | bytes 14155776 | tf_op jit(solution)/shard_map/all_to_all | solution.py:50
  131.1 109.9 %all-to-all-start.2 = ((bf16[1,4,768,1536]{3,1,0,2:T(4,128)(2,1)}), bf16[1,4,768,1536]{3,1,0,2:T(4,128)(2,1)}, u32[]{:S(2)}, u32[]{:S(2)}) async-start(bf16[1,4,768,1536]{3,1,0,2:T(4,128)(2,1)} %copy.149), calls=%async_computation.2 | async-start | bytes 18874368 | tf_op jit(solution)/shard_map/all_to_all | solution.py:50
  240.9 109.9 %all-to-all-start.3 = ((bf16[1,4,1536,768]{3,1,0,2:T(4,128)(2,1)}), bf16[1,4,1536,768]{3,1,0,2:T(4,128)(2,1)}, u32[]{:S(2)}, u32[]{:S(2)}) async-start(bf16[1,4,1536,768]{3,1,0,2:T(4,128)(2,1)} %copy.148), calls=%async_computation.3 | async-start | bytes 18874368 | tf_op jit(solution)/shard_map/all_to_all | solution.py:50
  246.7 239.0 %all-gather.7.cloned.1.call-start = ((), (), s32[]{:S(2)}) async-start(), calls=%async_computation.5 | async-start | bytes 2949120 | tf_op jit(solution)/shard_map/all_gather | solution.py:63
  248.1 1.2 copy-start.6
  256.6 14.3 %copy-start.2 = (f32[4,192,1152]{2,0,1:T(4,128)}, f32[4,192,1152]{2,0,1:T(4,128)S(1)}, u32[]{:S(2)}) copy-start(f32[4,192,1152]{2,0,1:T(4,128)S(1)} %convert_reduce_fusion.2) | copy-start | bytes 10616836
  270.9 2.2 copy-start
  360.8 2.2 copy-start.1
  363.0 40.0 %slice-start = ((s8[4718592]{0:T(1024)(128)(4,1)}), s8[524288]{0:T(1024)(128)(4,1)S(1)}, s32[]{:S(2)}) async-start(s8[4718592]{0:T(1024)(128)(4,1)} %bitcast.24), calls=%async_computation.8 | async-start | bytes 1048576
  391.1 11.9 %slice-start.1 = ((s8[4718592]{0:T(1024)(128)(4,1)}), s8[4194304]{0:T(1024)(128)(4,1)S(1)}, s32[]{:S(2)}) async-start(s8[4718592]{0:T(1024)(128)(4,1)} %bitcast.24), calls=%async_computation.9 | async-start | bytes 8388608
  403.0 12.0 %copy-start.3 = (f32[4,192,1152]{2,0,1:T(4,128)S(1)}, f32[4,192,1152]{2,0,1:T(4,128)}, u32[]{:S(2)}) copy-start(f32[4,192,1152]{2,0,1:T(4,128)} %copy-done.2) | copy-start | bytes 10616836
  403.0 12.0 %copy-start.4 = (f32[4,192,1152]{2,1,0:T(8,128)S(1)}, f32[4,192,1152]{2,1,0:T(8,128)}, u32[]{:S(2)}) copy-start(f32[4,192,1152]{2,1,0:T(8,128)} %param.17) | copy-start | bytes 10616836
  403.1 12.0 %copy-start.9 = (f32[4,192,1152]{2,1,0:T(8,128)S(1)}, f32[4,192,1152]{2,1,0:T(8,128)}, u32[]{:S(2)}) copy-start(f32[4,192,1152]{2,1,0:T(8,128)} %param.18) | copy-start | bytes 10616836
  403.1 12.0 %copy-start.10 = (f32[4,192,1152]{2,1,0:T(8,128)S(1)}, f32[4,192,1152]{2,1,0:T(8,128)}, u32[]{:S(2)}) copy-start(f32[4,192,1152]{2,1,0:T(8,128)} %param.19) | copy-start | bytes 10616836
  415.1 5.8 copy-start.7
  415.1 5.8 copy-start.8
  415.1 5.8 copy-start.11
  415.1 5.8 copy-start.12
  423.4 30.4 %copy-start.5 = (f32[4,192,1152]{2,1,0:T(8,128)S(1)}, f32[4,192,1152]{2,1,0:T(8,128)}, u32[]{:S(2)}) copy-start(f32[4,192,1152]{2,1,0:T(8,128)} %param.17) | copy-start | bytes 10616836
  447.7 5.9 copy-start.15
  453.4 72.4 %all-gather.5.cloned.1.call-start = ((), (), s32[]{:S(2)}) async-start(), calls=%async_computation.4 | async-start | bytes 8847360 | tf_op jit(solution)/shard_map/all_gather | solution.py:63
  460.5 2.7 copy-start.14
  463.1 126.6 %all-gather.11.cloned.1.call-start = ((), (), s32[]{:S(2)}) async-start(), calls=%async_computation.7 | async-start | bytes 11796480 | tf_op jit(solution)/shard_map/all_gather | solution.py:63
  471.0 3.6 copy-start.13
  474.3 179.2 %all-gather.9.cloned.1.call-start = ((), (), s32[]{:S(2)}) async-start(), calls=%async_computation.6 | async-start | bytes 11796480 | tf_op jit(solution)/shard_map/all_gather | solution.py:63
Sparse Core Ops, SparseCore 0:
  453.5 21.9 all-gather.6
  477.6 48.1 all-gather.4
  527.9 61.7 all-gather.10
  591.7 61.7 all-gather.8
where the time goes:
time: 678 us; the launch traced here: 670 us
  waiting for transfers between devices  375 us (55%)
  local copies, waits for them, and re-layouts  110 us (16%)
  other arithmetic  96.8 us (14%)
  blocking collectives  47.5 us (7%)
  starting transfers between devices  22.5 us (3%)
  between operations  17.8 us (3%)
    all_to_all x4, waiting for transfers between devices, device_step(): received = lax.all_to_all(sent_grad, 'data', 2, 0, tiled=True)  226 us
    all_gather x4, waiting for transfers between devices, device_step(): lax.all_gather(new_weight.astype(jnp.bfloat16), 'data', axis=1, tiled=True)  149 us
    unnamed x44, local copies, waits for them, and re-layouts  98.7 us
    reduce_sum x4, other arithmetic, device_step(): jnp.sum(weight * weight, axis=(1, 2))  32 us
    reduce_sum x4, other arithmetic, device_step(): grad_means.append(jnp.sum(received, axis=0, dtype=jnp.float32) / group_size)  29 us
    convert_element_type x4, other arithmetic, device_step(): new_weight.astype(jnp.bfloat16)  26.1 us
    psum x1, blocking collectives, device_step(): norm_pair = jnp.sqrt(lax.psum(sq_pair, ('model', 'data')))  24.4 us
    psum x1, blocking collectives, device_step(): total_norm = jnp.sqrt(lax.psum(local_sq, ('model', 'data')))  23.1 us
  transfers between devices with their start and end apart: 8, of which 7 were waited for; matrix products, arithmetic and copies ran while one was open for 20% of the time, Pallas kernels for 0%

commit v1 on v0

v1 whole, which is shorter than its diff:
```python
import functools

import jax
import jax.numpy as jnp
from jax import lax
from jax.experimental import pallas as pl
from jax.experimental.pallas import tpu as pltpu
from jax.sharding import PartitionSpec as P


LEARN_RATE = 0.08
BETA_ONE = 0.9
BETA_TWO = 0.999
ADAM_EPS = 1e-6
DECAY_RATE = 0.01
MAX_NORM = 1.0
STEP_COUNT = 100
COLUMN_SPLIT = (True, False, True, False)
MESH = pl.DeviceIdType.MESH
F32, BF16 = jnp.float32, jnp.bfloat16

UNIT_ROWS, UNIT_COLS = 96, 384
CHUNK = 16
PAIR = 2
TILE = (8, 128)
OWN, NEAR, FAR, CROSS = PARTNERS = range(4)
OTHERS = (NEAR, FAR, CROSS)
PROJ, QKV, FCIN, FCOUT = KINDS = range(4)
KIND_ORDER = (1, 0, 2, 3)
SHARD_ROWS = (96, 192, 192, 384)
SHARD_COLS = (768, 1152, 1536, 768)
LAYERS = 4
COL_BLOCKS = tuple(cols // UNIT_COLS for cols in SHARD_COLS)
BLOCKS = tuple(rows // UNIT_ROWS * (cols // UNIT_COLS) for rows, cols in zip(SHARD_ROWS, SHARD_COLS))
FIRST = tuple(sum(LAYERS * blocks for blocks in BLOCKS[:k]) for k in range(5))
UNITS = FIRST[-1]
GROUPS = UNITS // PAIR
RING = 16
SEND_SLOTS = 8
LAG = 8
RESIDENT = PAIR * RING
SENT_UNITS = FIRST[FCIN]
SENT_GROUPS = SENT_UNITS // PAIR
PIECE_UNITS = FIRST[FCOUT] - FIRST[FCIN]
LATE_GROUPS = 2
RELAYED = SENT_GROUPS - LATE_GROUPS
LAST_ROWS = 192
PIECES = tuple(
    [(layer, 0, SHARD_ROWS[kind]) for layer in range(LAYERS - (kind == FCOUT))]
    + [(LAYERS - 1, 0, SHARD_ROWS[kind] - LAST_ROWS), (LAYERS - 1, SHARD_ROWS[kind] - LAST_ROWS, LAST_ROWS)] * (kind == FCOUT)
    for kind in (FCIN, FCOUT))
PIECE_COUNT = sum(map(len, PIECES))


def grad_spec(col_split):
    return P("data", None, None, "model") if col_split else P("data", None, "model", None)


def state_spec(col_split):
    return P(None, "data", "model") if col_split else P(None, ("model", "data"), None)


def replica_spec(col_split):
    return P(None, None, "model") if col_split else P(None, "model", None)


def adam_direction(grad_mean, weight, moment1, moment2, clip_coef):
    clipped = clip_coef * grad_mean
    new_first = BETA_ONE * moment1 + (1.0 - BETA_ONE) * clipped
    new_second = BETA_TWO * moment2 + (1.0 - BETA_TWO) * clipped * clipped
    first_hat = new_first / (1.0 - BETA_ONE ** STEP_COUNT)
    second_hat = new_second / (1.0 - BETA_TWO ** STEP_COUNT)
    update = first_hat / (jnp.sqrt(second_hat) + ADAM_EPS) + DECAY_RATE * weight
    return update, new_first, new_second


def fold(x):
    sublanes, lanes = TILE
    parts = [x[i:i + sublanes, j:j + lanes] for i in range(0, CHUNK, sublanes) for j in range(0, UNIT_COLS, lanes)]
    return functools.reduce(jnp.add, parts)


def pair(group):
    return pl.ds(PAIR * group, PAIR)


def partners(data):
    return data, data + 1 - PAIR * (data % PAIR), (data + PAIR) % len(PARTNERS), CROSS - data


def zeros():
    return jnp.zeros(TILE, F32)


def split(items, *counts):
    items = iter(items)
    return [[next(items) for _ in range(count)] for count in counts]


def place(kind, index):
    blocks, col_blocks = BLOCKS[kind], COL_BLOCKS[kind]
    layer, block = index // blocks, index % blocks
    row = pl.multiple_of(block // col_blocks * UNIT_ROWS, UNIT_ROWS)
    col = pl.multiple_of(block % col_blocks * UNIT_COLS, UNIT_COLS)
    return layer, row, col


def for_kind(unit, kinds, body):
    for kind in kinds:
        @pl.when((unit >= FIRST[kind]) & (unit < FIRST[kind + 1]))
        def _():
            body(kind, unit - FIRST[kind])


def step_kernel(*refs):
    counts = tuple(map(len, PIECES))
    grads, weights, firsts, seconds, means, reps, in_pieces, out_pieces, rest = split(refs, *[len(KINDS)] * 5, PAIR, *counts, 20)
    pieces = {FCIN: in_pieces, FCOUT: out_pieces}
    (late, scal_out, recv, stage, mean, held, ring, note, notes, w_sums, u_sums, n_sum, scal,
     ring_sem, held_sem, mean_sem, send_sem, recv_sem, rep_send_sem, note_sem) = rest
    model, data = lax.axis_index("model"), lax.axis_index("data")
    partner = partners(data)

    def unit_at(ref, kind, index, quarter_base=None):
        layer, row, col = place(kind, index)
        if quarter_base is not None:
            row = pl.multiple_of(quarter_base * SHARD_ROWS[kind] + row, UNIT_ROWS)
            return ref.at[layer, pl.ds(row, UNIT_ROWS), pl.ds(col, UNIT_COLS)]
        return ref.at[layer, pl.ds(row, UNIT_ROWS), pl.ds(col, UNIT_COLS)]

    def start_grads(unit):
        def body(kind, index):
            for k in PARTNERS:
                pltpu.make_async_copy(unit_at(grads[kind].at[0], kind, index, partner[k]), ring.at[unit % RING, k], ring_sem.at[unit % RING]).start()

        for_kind(unit, KINDS, body)

    def start_moments(unit, kinds):
        slot, part = unit // PAIR % RING, PAIR * (unit % PAIR)

        def body(kind, index):
            pltpu.make_async_copy(unit_at(firsts[kind], kind, index), ring.at[slot, part], ring_sem.at[slot]).start()
            pltpu.make_async_copy(unit_at(seconds[kind], kind, index), ring.at[slot, part + 1], ring_sem.at[slot]).start()

        for_kind(unit, kinds, body)

    def start_weight(unit):
        def body(kind, index):
            pltpu.make_async_copy(unit_at(weights[kind], kind, index), held.at[unit], held_sem.at[unit // PAIR % RING]).start()

        for_kind(unit, KINDS, body)

    def start_mean_out(unit):
        def body(kind, index):
            pltpu.make_async_copy(mean.at[unit], unit_at(means[kind], kind, index), mean_sem.at[unit // PAIR % SEND_SLOTS]).start()

        for_kind(unit, KINDS, body)

    def block(ref, count):
        return ref.at[pl.ds(0, count), pl.ds(0, UNIT_ROWS), pl.ds(0, UNIT_COLS)]

    def wait_ring(slot):
        pltpu.make_async_copy(block(grads[QKV].at[0], len(PARTNERS)), ring.at[slot], ring_sem.at[slot]).wait()

    def wait_weights(group):
        pltpu.make_async_copy(block(weights[QKV], PAIR), held.at[pair(group)], held_sem.at[group % RING]).wait()

    def wait_mean_out(group):
        pltpu.make_async_copy(mean.at[pair(group)], block(means[QKV], PAIR), mean_sem.at[group % SEND_SLOTS]).wait()

    def landed(count):
        return recv.at[0, pl.ds(0, count)]

    def remote(source, target, sent, received, k):
        return pltpu.make_async_remote_copy(source, target, sent, received, device_id=(model, partner[k]), device_id_type=MESH)

    def stage_slot(group, k):
        return group % SEND_SLOTS * len(OTHERS) + k - 1

    def grad_copy(group, k):
        return remote(stage.at[pair(stage_slot(group, k))], recv.at[k - 1, pair(group)], send_sem.at[group % SEND_SLOTS], recv_sem.at[group], k)

    def grad_copies(group):
        count = len(OTHERS) * PAIR
        return remote(landed(count), landed(count), send_sem.at[group % SEND_SLOTS], recv_sem.at[group], FAR)

    early = PAIR * PAIR
    for unit in range(early):
        start_grads_static(unit, grads, ring, ring_sem, partner)

    barrier = pltpu.get_barrier_semaphore()
    peers = [(side, k) for k in (FAR, CROSS, OWN, NEAR) for side in (1, 0) if side or k]

    def device(peer):
        return (model + peer[0]) % PAIR, partner[peer[1]]

    for peer in peers:
        pl.semaphore_signal(barrier, inc=1, device_id=device(peer), device_id_type=MESH)
    pl.semaphore_wait(barrier, len(peers))
    for unit in range(early, RING):
        start_grads_static(unit, grads, ring, ring_sem, partner)

    n_sum[...] = jnp.zeros_like(n_sum)
    note[...] = jnp.zeros_like(note)
    w_sums[...] = jnp.zeros_like(w_sums)
    u_sums[...] = jnp.zeros_like(u_sums)

    def convert(group):
        for j in range(PAIR):
            unit = PAIR * group + j
            wait_ring(unit % RING)

            def rows(i, _):
                at = pl.ds(pl.multiple_of(i * CHUNK, CHUNK), CHUNK)
                for k in OTHERS:
                    stage[PAIR * stage_slot(group, k) + j, at, :] = ring[unit % RING, k, at, :].astype(BF16)
                return 0

            lax.fori_loop(0, UNIT_ROWS // CHUNK, rows, 0)

    def keep_own(group):
        for j in range(PAIR):
            unit = PAIR * group + j

            def rows(i, _):
                at = pl.ds(pl.multiple_of(i * CHUNK, CHUNK), CHUNK)
                mean[unit, at, :] = ring[unit % RING, OWN, at, :].astype(BF16).astype(F32)
                return 0

            lax.fori_loop(0, UNIT_ROWS // CHUNK, rows, 0)

    def add_up(group):
        grad_copies(group).wait_recv()
        wait_weights(group)

        @pl.when(group >= SEND_SLOTS)
        def _():
            wait_mean_out(group - SEND_SLOTS)

        for j in range(PAIR):
            unit = PAIR * group + j

            def rows(i, sums):
                at = pl.ds(pl.multiple_of(i * CHUNK, CHUNK), CHUNK)
                near, far, cross = (recv[k - 1, unit, at, :].astype(F32) for k in OTHERS)
                total = (mean[unit, at, :] + near + (far + cross)) / len(PARTNERS)
                mean[unit, at, :] = total
                weight = held[unit, at, :]
                g_sum, w_sum = sums
                return g_sum + fold(total * total), w_sum + fold(weight * weight)

            g_part, w_part = lax.fori_loop(0, UNIT_ROWS // CHUNK, rows, (zeros(), zeros()))
            n_sum[...] += g_part

            def body(kind, index):
                tensor = LAYERS * kind + index // BLOCKS[kind]
                w_sums[tensor] += w_part

            for_kind(unit, KINDS, body)
            start_mean_out(unit)

    def exchange_step(group, _):
        for j in range(PAIR):
            start_weight(PAIR * group + j)

        @pl.when(group >= SEND_SLOTS)
        def _():
            grad_copies(group - SEND_SLOTS).wait_send()

        convert(group)
        keep_own(group)
        for k in (FAR, CROSS, NEAR):
            grad_copy(group, k).start()

        for j in range(PAIR):
            unit = PAIR * group + j

            @pl.when(unit + RING < UNITS)
            def _():
                start_grads(unit + RING)

            @pl.when(unit + RING >= UNITS)
            def _():
                for other in range(PAIR):
                    start_moments(PAIR * (unit + RING - UNITS) + other, (PROJ, QKV))

        @pl.when(group >= LAG + 1)
        def _():
            add_up(group - LAG - 1)

        return 0

    lax.fori_loop(0, GROUPS, exchange_step, 0)

    def drain_step(group, _):
        add_up(group)
        return 0

    lax.fori_loop(GROUPS - LAG - 1, GROUPS, drain_step, 0)

    n_note, early_note = len(KINDS), len(KINDS) + 1

    def rows_of(index):
        return pl.ds(0, TILE[0] if index in (n_note, early_note) else 1)

    def send_note(index):
        for slot, peer in enumerate(peers):
            pltpu.make_async_remote_copy(
                note.at[index, rows_of(index)], notes.at[index, slot, rows_of(index)], note_sem.at[0, index], note_sem.at[1, index],
                device_id=device(peer), device_id_type=MESH).start()

    def read_note(index):
        arrived = notes.at[index, pl.ds(0, len(peers)), rows_of(index)]
        remote(arrived, arrived, note_sem.at[0, index], note_sem.at[1, index], FAR).wait()
        return note[index] + jnp.sum(notes[index], axis=0)

    note[n_note] = n_sum[...]

    def settle(group, _):
        grad_copies(group).wait_send()
        return 0

    lax.fori_loop(GROUPS - SEND_SLOTS, GROUPS, settle, 0)
    send_note(n_note)

    def settle_means(group, _):
        wait_mean_out(group)
        return 0

    lax.fori_loop(GROUPS - SEND_SLOTS, GROUPS, settle_means, 0)
    total_sq = jnp.sum(jnp.sum(read_note(n_note), axis=0, keepdims=True), axis=1, keepdims=True)
    clip = jnp.minimum(1.0, MAX_NORM / jnp.sqrt(total_sq))
    scal[len(KINDS)] = jnp.broadcast_to(clip, TILE)

    def directions(kind, unit_from, unit_to):
        def group_step(index, _):
            group = FIRST[kind] // PAIR + index
            slot = group % RING
            wait_ring(slot)
            total = zeros()
            for j in range(PAIR):
                unit, part = PAIR * group + j, PAIR * j
                for i in range(0, UNIT_ROWS, CHUNK):
                    at = pl.ds(i, CHUNK)
                    update, _, _ = adam_direction(mean[unit, at, :], held[unit, at, :], ring[slot, part, at, :], ring[slot, part + 1, at, :], clip)
                    mean[unit, at, :] = update
                    total = total + fold(update * update)
            u_sums[LAYERS * kind + PAIR * index // BLOCKS[kind]] += total
            return 0

        lax.fori_loop(unit_from // PAIR, unit_to // PAIR, group_step, 0)

    def refill(unit_from, unit_to):
        def unit_step(unit, _):
            start_moments(unit + RESIDENT, (FCIN, FCOUT))
            return 0

        lax.fori_loop(unit_from, unit_to, unit_step, 0)

    def tensor_sums(kind, layers):
        return [jnp.sum(sums[LAYERS * kind + layer], axis=0, keepdims=True) for sums in (u_sums, w_sums) for layer in range(layers)]

    def write_early_note():
        for row, total in zip((0, LAYERS), tensor_sums(PROJ, 1)):
            note[early_note, row:row + 1, :] = total

    def write_note(kind):
        lane = lax.broadcasted_iota(jnp.int32, (1, TILE[1]), 1)
        packed = jnp.zeros((1, TILE[1]), F32)
        for index, total in enumerate(tensor_sums(kind, LAYERS)):
            packed = jnp.where(lane == index, jnp.sum(total, axis=1, keepdims=True), packed)
        note[kind, :1, :] = packed

    def early_ratio():
        norms = jnp.sqrt(jnp.sum(read_note(early_note), axis=1, keepdims=True))
        scal[PROJ, :1, :] = jnp.broadcast_to(norms[LAYERS:LAYERS + 1] / norms[:1], (1, TILE[1]))

    def ratios(kind):
        norms = jnp.sqrt(read_note(kind)[:1, :])
        for layer in range(LAYERS):
            ratio = norms[:, LAYERS + layer:LAYERS + layer + 1] / norms[:, layer:layer + 1]
            scal[kind, layer:layer + 1, :] = jnp.broadcast_to(ratio, (1, TILE[1]))

    def new_weights(kind, unit_from, unit_to, target):
        def unit_step(index, _):
            unit = FIRST[kind] + index
            ratio = LEARN_RATE * scal[kind, pl.ds(index // BLOCKS[kind], 1), :][:, :1]
            for i in range(0, UNIT_ROWS, CHUNK):
                at = pl.ds(i, CHUNK)
                target[unit, at, :] = (held[unit, at, :] - ratio * mean[unit, at, :]).astype(BF16)
            return 0

        lax.fori_loop(unit_from, unit_to, unit_step, 0)

    near_sem = PAIR * SENT_GROUPS

    def rep_copy(group, k):
        source = recv.at[FAR - 1, pair(group)] if k == CROSS else stage.at[pair(group)]
        arrival = {NEAR: near_sem, FAR: group, CROSS: SENT_GROUPS + group}[k]
        return remote(source, recv.at[k - 1, pair(group)], rep_send_sem.at[k - 1], recv_sem.at[arrival], FAR if k == FAR else NEAR)

    def late_copy(group):
        return remote(stage.at[pair(group)], late.at[pair(group - RELAYED)], rep_send_sem.at[FAR - 1], recv_sem.at[group], FAR)

    def all_copies(k, count):
        return remote(landed(count), landed(count), rep_send_sem.at[k - 1], recv_sem.at[near_sem], NEAR)

    def start_replicas(unit_from, unit_to):
        def body(group, _):
            @pl.when(group < RELAYED)
            def _():
                rep_copy(group, FAR).start()

            @pl.when(group >= RELAYED)
            def _():
                late_copy(group).start()

            rep_copy(group, NEAR).start()
            return 0

        lax.fori_loop(unit_from // PAIR, unit_to // PAIR, body, 0)

    def replicas_out(unit_from, unit_to, k):
        def unit_step(unit, _):
            def body(kind, index):
                source = recv.at[k - 1, unit] if k else stage.at[unit]
                pltpu.make_async_copy(source, unit_at(reps[kind], kind, index, partner[k]), mean_sem.at[k]).start()

            for_kind(unit, (PROJ, QKV), body)
            return 0

        lax.fori_loop(unit_from, unit_to, unit_step, 0)

    def pieces_out(kind):
        for ref, (layer, first, rows) in zip(pieces[kind], PIECES[kind - FCIN]):
            for row in range(0, rows, UNIT_ROWS):
                for column in range(COL_BLOCKS[kind]):
                    unit = FIRST[kind] + layer * BLOCKS[kind] + (first + row) // UNIT_ROWS * COL_BLOCKS[kind] + column
                    target = ref.at[0, pl.ds(row, UNIT_ROWS), pl.ds(column * UNIT_COLS, UNIT_COLS)]
                    pltpu.make_async_copy(recv.at[0, unit], target, mean_sem.at[PAIR + kind]).start()

    proj_end, qkv_end, piece_end = (FIRST[kind + 1] - FIRST[kind] for kind in (PROJ, QKV, FCIN))
    first, half = BLOCKS[PROJ], qkv_end // PAIR
    directions(PROJ, 0, first)
    write_early_note()
    refill(0, first)
    send_note(early_note)
    directions(PROJ, first, proj_end)
    write_note(PROJ)
    directions(QKV, 0, PAIR)
    send_note(PROJ)
    directions(QKV, PAIR, half)
    early_ratio()
    new_weights(PROJ, 0, first, stage)
    refill(first, PAIR * first)
    start_replicas(0, first)
    ratios(PROJ)
    new_weights(PROJ, first, proj_end, stage)
    directions(QKV, half, qkv_end)
    start_replicas(first, PAIR * first)
    write_note(QKV)
    refill(PAIR * first, SENT_UNITS)
    send_note(QKV)
    start_replicas(PAIR * first, proj_end)
    directions(FCIN, 0, piece_end // PAIR)
    ratios(QKV)
    new_weights(QKV, 0, half, stage)
    directions(FCIN, piece_end // PAIR, piece_end // PAIR + PAIR)
    start_replicas(proj_end, proj_end + half)
    directions(FCIN, piece_end // PAIR + PAIR, piece_end)
    refill(FIRST[FCIN], FIRST[FCOUT])
    new_weights(QKV, half, qkv_end, stage)
    directions(FCOUT, 0, piece_end)
    write_note(FCIN)
    write_note(FCOUT)
    replicas_out(0, SENT_UNITS, OWN)
    send_note(FCIN)
    send_note(FCOUT)
    start_replicas(proj_end + half, SENT_UNITS)
    for kind in (FCIN, FCOUT):
        ratios(kind)
        new_weights(kind, 0, piece_end, recv.at[0])
    scal_copy = pltpu.make_async_copy(scal, scal_out, mean_sem.at[len(KINDS) + PAIR])
    scal_copy.start()
    pieces_out(FCIN)
    pieces_out(FCOUT)

    def relay_step(group, _):
        @pl.when(group < RELAYED)
        def _():
            rep_copy(group, FAR).wait_recv()
            rep_copy(group, CROSS).start()
            replicas_out(PAIR * group, PAIR * group + PAIR, FAR)

        @pl.when(group >= 1)
        def _():
            rep_copy(group - 1, CROSS).wait_recv()
            replicas_out(PAIR * group - PAIR, PAIR * group, CROSS)

        return 0

    lax.fori_loop(0, RELAYED + 1, relay_step, 0)
    all_copies(NEAR, SENT_UNITS).wait()
    replicas_out(0, SENT_UNITS, NEAR)
    all_copies(FAR, SENT_UNITS).wait_send()
    all_copies(CROSS, PAIR * RELAYED).wait_send()
    for index, count in enumerate((SENT_UNITS, SENT_UNITS, PAIR * RELAYED, PAIR * RELAYED, PIECE_UNITS, PIECE_UNITS)):
        pltpu.make_async_copy(landed(count), landed(count), mean_sem.at[index]).wait()
    scal_copy.wait()
    for group in range(RELAYED, SENT_GROUPS):
        late_copy(group).wait_recv()


def place_static(kind, index):
    block = index % BLOCKS[kind]
    return index // BLOCKS[kind], block // COL_BLOCKS[kind] * UNIT_ROWS, block % COL_BLOCKS[kind] * UNIT_COLS


def start_grads_static(unit, grads, ring, ring_sem, partner):
    kind = next(kind for kind in KINDS if unit < FIRST[kind + 1])
    layer, row, col = place_static(kind, unit - FIRST[kind])
    for k in PARTNERS:
        base = pl.multiple_of(partner[k] * SHARD_ROWS[kind] + row, UNIT_ROWS)
        pltpu.make_async_copy(grads[kind].at[0, layer, pl.ds(base, UNIT_ROWS), pl.ds(col, UNIT_COLS)], ring.at[unit, k], ring_sem.at[unit]).start()


def assemble_kernel(*refs):
    (proj, qkv, late, late_near), own, near, outs, scratch = split(refs, len(KINDS), PIECE_COUNT, PIECE_COUNT, len(KINDS), 7)
    proj_buf, qkv_buf, in_buf, out_buf, late_sem, whole_sem, piece_sem = scratch
    partner = partners(lax.axis_index("data"))
    copies = []

    def through(source, buffer, target, sem):
        copies.append((pltpu.make_async_copy(source, buffer, sem.at[0]), pltpu.make_async_copy(buffer, target, sem.at[1])))

    for layer in range(LAYERS):
        through(qkv.at[layer], qkv_buf.at[layer], outs[QKV].at[layer], whole_sem.at[layer])
    through(proj, proj_buf, outs[PROJ], whole_sem.at[LAYERS])
    order = [(kind, piece) for kind in (FCIN, FCOUT) for piece in PIECES[kind - FCIN]]
    for number, (kind, (layer, first, rows)) in enumerate(order):
        for k, piece in ((OWN, own[number]), (NEAR, near[number])):
            at = (in_buf if kind == FCIN else out_buf).at[k, pl.ds(layer, 1), pl.ds(first, rows)]
            base = pl.multiple_of(partner[k] * SHARD_ROWS[kind] + first, UNIT_ROWS)
            through(piece, at, outs[kind].at[pl.ds(layer, 1), pl.ds(base, rows)], piece_sem.at[k, number])
    for fetch, _ in copies:
        fetch.start()
    for position, (fetch, store) in enumerate(copies):
        fetch.wait()
        if position == LAYERS - 1:
            fills = []
            for k, source in ((FAR, late), (CROSS, late_near)):
                for unit in range(PAIR * LATE_GROUPS):
                    layer, row, col = place_static(QKV, PAIR * RELAYED + unit - FIRST[QKV])
                    base = pl.multiple_of(partner[k] * SHARD_ROWS[QKV] + row, UNIT_ROWS)
                    target = qkv_buf.at[layer, pl.ds(base, UNIT_ROWS), pl.ds(col, UNIT_COLS)]
                    fills.append(pltpu.make_async_copy(source.at[unit], target, late_sem.at[k - FAR, unit]))
            for fill in fills:
                fill.start()
            for fill in fills:
                fill.wait()
        store.start()
    for _, store in copies:
        store.wait()


def assemble(reps, late, late_near, own, near):
    shape, dma = jax.ShapeDtypeStruct, pltpu.SemaphoreType.DMA
    whole = [(LAYERS, len(PARTNERS) * rows, cols) for rows, cols in zip(SHARD_ROWS, SHARD_COLS)]
    any_spec = pl.BlockSpec(memory_space=pl.ANY)
    operands = [*reps, late, late_near, *own, *near]
    return pl.pallas_call(
        assemble_kernel,
        out_shape=[shape(s, BF16) for s in whole],
        in_specs=[any_spec] * len(operands),
        out_specs=[any_spec] * len(whole),
        scratch_shapes=[
            pltpu.VMEM(whole[PROJ], BF16),
            pltpu.VMEM(whole[QKV], BF16),
            pltpu.VMEM((PAIR, LAYERS, SHARD_ROWS[FCIN], SHARD_COLS[FCIN]), BF16),
            pltpu.VMEM((PAIR, LAYERS, SHARD_ROWS[FCOUT], SHARD_COLS[FCOUT]), BF16),
            dma((PAIR, PAIR * LATE_GROUPS)), dma((LAYERS + 1, PAIR)), dma((PAIR, len(own), PAIR)),
        ],
        compiler_params=pltpu.CompilerParams(vmem_limit_bytes=24_000_000),
        cost_estimate=pl.CostEstimate(flops=12_000_000, bytes_accessed=38_000_000, transcendentals=0),
    )(*operands)


def solution(mesh):
    in_specs = []
    for col_split in COLUMN_SPLIT:
        in_specs.extend([grad_spec(col_split), state_spec(col_split), state_spec(col_split), state_spec(col_split)])
    out_specs = tuple([replica_spec(col_split) for col_split in COLUMN_SPLIT] + [state_spec(col_split) for col_split in COLUMN_SPLIT] * 3)
    across, beside = ([(i, partners(i)[k]) for i in PARTNERS] for k in (FAR, NEAR))

    def device_step(*arrays):
        shape = jax.ShapeDtypeStruct
        shard = [(LAYERS, rows, cols) for rows, cols in zip(SHARD_ROWS, SHARD_COLS)]
        order = [(kind, piece) for kind in (FCIN, FCOUT) for piece in PIECES[kind - FCIN]]
        scal_shape = (len(KINDS) + 1,) + TILE
        out_shape = (
            [shape(s, F32) for s in shard]
            + [shape((LAYERS, len(PARTNERS) * SHARD_ROWS[kind], SHARD_COLS[kind]), BF16) for kind in (PROJ, QKV)]
            + [shape((1, rows, SHARD_COLS[kind]), BF16) for kind, (_, _, rows) in order]
            + [shape((PAIR * LATE_GROUPS, UNIT_ROWS, UNIT_COLS), BF16), shape(scal_shape, F32)])
        any_spec = pl.BlockSpec(memory_space=pl.ANY)
        dma = pltpu.SemaphoreType.DMA
        unit = (UNIT_ROWS, UNIT_COLS)
        messages = len(KINDS) + PAIR
        operands = [arrays[len(KINDS) * kind + part] for part in PARTNERS for kind in KIND_ORDER]
        results = pl.pallas_call(
            step_kernel,
            out_shape=out_shape,
            in_specs=[any_spec] * len(operands),
            out_specs=[any_spec] * len(out_shape),
            scratch_shapes=[
                pltpu.VMEM((len(OTHERS), UNITS) + unit, BF16),
                pltpu.VMEM((len(OTHERS) * PAIR * SEND_SLOTS,) + unit, BF16),
                pltpu.VMEM((UNITS,) + unit, F32),
                pltpu.VMEM((UNITS,) + unit, F32),
                pltpu.VMEM((RING, len(PARTNERS)) + unit, F32),
                pltpu.VMEM((messages,) + TILE, F32),
                pltpu.VMEM((messages, mesh.size - 1) + TILE, F32),
                pltpu.VMEM((LAYERS * len(KINDS),) + TILE, F32),
                pltpu.VMEM((LAYERS * len(KINDS),) + TILE, F32),
                pltpu.VMEM(TILE, F32),
                pltpu.VMEM(scal_shape, F32),
                dma((RING,)), dma((RING,)), dma((SEND_SLOTS,)), dma((SEND_SLOTS,)), dma((GROUPS,)), dma((len(OTHERS),)), dma((PAIR, messages)),
            ],
            compiler_params=pltpu.CompilerParams(collective_id=0, has_side_effects=True, vmem_limit_bytes=66_900_000),
        )(*operands)
        means, reps, pieces, (late, scal) = split(results, len(KINDS), PAIR, PIECE_COUNT, PAIR)
        owners = partners(lax.axis_index("data"))
        state = {}
        clip = scal[len(KINDS), 0, 0]
        for slot, kind in enumerate(KIND_ORDER):
            _, weight, moment1, moment2 = arrays[len(KINDS) * kind:len(KINDS) * kind + len(KINDS)]
            update, new_first, new_second = adam_direction(means[slot], weight, moment1, moment2, clip)
            ratio = jnp.expand_dims(scal[slot, :LAYERS, 0], (1, 2))
            state[kind] = (weight - LEARN_RATE * ratio * update, new_first, new_second)
        far, near = [], []
        for piece in pieces:
            far.append(lax.ppermute(piece, "data", across))
        late_near = lax.ppermute(late, "data", beside)
        near = [lax.ppermute(piece, "data", beside) for piece in pieces]
        replicas = list(assemble(reps, late, late_near, pieces, near))
        for number, (kind, (layer, first, _)) in enumerate(order):
            far_near = lax.ppermute(far[number], "data", beside)
            for piece, k in ((far[number], FAR), (far_near, CROSS)):
                replicas[kind] = lax.dynamic_update_slice(replicas[kind], piece, (layer, owners[k] * SHARD_ROWS[kind] + first, 0))
        outputs = [replicas[KIND_ORDER.index(kind)] for kind in KINDS]
        return tuple(outputs + [state[kind][part] for part in range(len(OTHERS)) for kind in KINDS])

    return jax.shard_map(device_step, mesh=mesh, in_specs=tuple(in_specs), out_specs=out_specs, check_vma=False)
```

time: 678 us -> 533 us (0.79); the launches traced: 670 us -> 532 us
  Pallas kernels: 0 us -> 381 us
  waiting for transfers between devices: 375 us -> 54.5 us
  local copies, waits for them, and re-layouts: 110 us -> 45.6 us
  other arithmetic: 96.8 us -> 37.7 us
  blocking collectives: 47.5 us -> 0 us
  between operations: 17.8 us -> 0.85 us
  starting transfers between devices: 22.5 us -> 12.1 us
    pallas_call x0 -> x2, Pallas kernels: none -> 381 us  [the longest x1 371 us: device_step(): pl.pallas_call(step_kernel, out_shape=out_shape, in_specs=[any_spec] * le...]
    all_to_all x4 -> x0, waiting for transfers between devices: 226 us -> none  [device_step(): received = lax.all_to_all(sent_grad, 'data', 2, 0, tiled=True)]
    all_gather x4 -> x0, waiting for transfers between devices: 149 us -> none  [device_step(): lax.all_gather(new_weight.astype(jnp.bfloat16), 'data', axis=1, tiled=True)]
    unnamed x44 -> x72, local copies, waits for them, and re-layouts: 98.7 us -> 23.1 us
    reduce_sum x12 -> x0, other arithmetic: 70.7 us -> none  [the longest x4 32 us: device_step(): jnp.sum(weight * weight, axis=(1, 2))]
    ppermute x0 -> x28, waiting for transfers between devices: none -> 54.5 us  [the longest x9 54.4 us: device_step(): far.append(lax.ppermute(piece, 'data', across))]
    psum x2 -> x0, blocking collectives: 47.5 us -> none  [the longest x1 24.4 us: device_step(): norm_pair = jnp.sqrt(lax.psum(sq_pair, ('model', 'data')))]
    sub x0 -> x4, other arithmetic: none -> 36.8 us  [device_step(): state[kind] = (weight - LEARN_RATE * ratio * update, new_first, new_second)]
  transfers between devices with their start and end apart: 8 -> 28, of which waited for: 7 -> 3; matrix products, arithmetic and copies ran while one was open for 20% -> 11% of each run, Pallas kernels for 0% -> 2%
where the time goes in v1:
time: 533 us; the launch traced here: 532 us
  Pallas kernels  381 us (71%)
  waiting for transfers between devices  54.5 us (10%)
  local copies, waits for them, and re-layouts  45.6 us (9%)
  other arithmetic  37.7 us (7%)
  starting transfers between devices  12.1 us (2%)
    pallas_call x1, Pallas kernels, device_step(): pl.pallas_call(step_kernel, out_shape=out_shape, in_specs=[any_spec] * le...  371 us
    ppermute x9, waiting for transfers between devices, device_step(): far.append(lax.ppermute(piece, 'data', across))  54.4 us
    sub x4, other arithmetic, device_step(): state[kind] = (weight - LEARN_RATE * ratio * update, new_first, new_second)  36.8 us
    unnamed x72, local copies, waits for them, and re-layouts  23.1 us
    dynamic_update_slice x18, local copies, waits for them, and re-layouts, device_step(): lax.dynamic_update_slice(replicas[kind], piece, (layer, owners[k] * SHARD...  21.3 us
  transfers between devices with their start and end apart: 28, of which 3 were waited for; matrix products, arithmetic and copies ran while one was open for 11% of the time, Pallas kernels for 2%

profile of v1, /device:TPU:0, one launch (start us, length us, event | category | flops | bytes accessed | tf_op | source)
XLA Modules:
  0.0 532.0 jit_solution(3460739487616782662)
XLA Ops:
  0.6 370.8 %shard_map.279 = (f32[4,96,768]{2,1,0:T(8,128)}, f32[4,192,1152]{2,1,0:T(8,128)}, f32[4,192,1536]{2,1,0:T(8,128)}, f32[4,384,768]{2,1,0:T(8,128)}, bf16[4,384,76...) custom-call(f32[1,4,384,768]{3,2,1,0:T(8,128)} %refs_0_.1, ...), custom_call_target="tpu_custom_call" | custom-call | tf_op jit(solution)/shard_map/pallas_call | solution.py:610
  373.3 1.3 slice.16
  374.6 13.8 %multiply_subtract_fusion.1 = (f32[4,192,1536]{2,1,0:T(8,128)}, f32[4,192,1536]{2,1,0:T(8,128)}, f32[4,192,1536]{2,1,0:T(8,128)}) fusion(f32[4,192,1536]{2,1,0:T(8,128)} %refs_6_.1, f32[4]{0:T(128)S(1)} %get-tuple-element.59, f32[4,192,1536]{2,1,0:T(8,128)} %get-tuple-element.56, f32[]{:T(128)} %bitcast, f32[4,192,1536]{2,1,0:T(8,128)} %refs_10_.1, ...), kind=kLoop, calls=%fused_computation.7 | loop fusion | flops 18874368 | bytes 33030164 | tf_op jit(solution)/shard_map/sub | solution.py:639
  390.9 9.5 %multiply_subtract_fusion.2 = (f32[4,192,1152]{2,1,0:T(8,128)}, f32[4,192,1152]{2,1,0:T(8,128)}, f32[4,192,1152]{2,1,0:T(8,128)}) fusion(f32[4,192,1152]{2,1,0:T(8,128)S(1)} %copy-done.33, f32[4]{0:T(128)S(1)} %get-tuple-element.61, f32[4,192,1152]{2,1,0:T(8,128)} %get-tuple-element.54, f32[]{:T(128)} %bitcast, f32[4,192,1152]{2,1,0:T(8,128)} %refs_9_.1, ...), kind=kLoop, calls=%fused_computation.10 | loop fusion | flops 14155776 | bytes 24772628 | tf_op jit(solution)/shard_map/sub | solution.py:639
  402.0 1.4 collective-permute-start.20
  405.7 8.9 %multiply_subtract_fusion = (f32[4,384,768]{2,1,0:T(8,128)}, f32[4,384,768]{2,1,0:T(8,128)}, f32[4,384,768]{2,1,0:T(8,128)}) fusion(f32[4,384,768]{2,1,0:T(8,128)S(1)} %copy-done.30, f32[4]{0:T(128)S(1)} %get-tuple-element.58, f32[4,384,768]{2,1,0:T(8,128)} %get-tuple-element.57, f32[]{:T(128)} %bitcast, f32[4,384,768]{2,1,0:T(8,128)S(1)} %copy-done.31, ...), kind=kLoop, calls=%fused_computation.5 | loop fusion | flops 18874368 | bytes 33030164 | tf_op jit(solution)/shard_map/sub | solution.py:639
  415.4 1.4 collective-permute-start.22
  417.0 12.4 %collective-permute-done.20 = bf16[1,384,768]{2,1,0:T(8,128)(2,1)} collective-permute-done((bf16[1,384,768]{2,1,0:T(8,128)(2,1)S(1)}, bf16[1,384,768]{2,1,0:T(8,128)(2,1)}, u32[]{:S(2)}, u32[]{:S(2)}) %collective-permute-start.20) | collective-permute-done | bytes 589856 | tf_op jit(solution)/shard_map/ppermute | solution.py:642
  429.4 4.7 multiply_subtract_fusion.3
  434.7 7.3 %collective-permute-done.10 = bf16[1,192,1536]{2,1,0:T(8,128)(2,1)} collective-permute-done((bf16[1,192,1536]{2,1,0:T(8,128)(2,1)}, bf16[1,192,1536]{2,1,0:T(8,128)(2,1)}, u32[]{:S(2)}, u32[]{:S(2)}) %collective-permute-start.10) | collective-permute-done | bytes 589856 | tf_op jit(solution)/shard_map/ppermute | solution.py:642
  442.0 3.0 copy-done
  445.0 1.1 copy-done.4
  446.1 1.1 copy-done.6
  447.2 1.1 copy-done.8
  448.2 1.1 copy-done.10
  449.3 1.1 copy-done.12
  450.4 1.1 copy-done.14
  451.4 1.1 copy-done.16
  452.5 1.1 copy-done.18
  453.6 1.1 copy-done.20
  455.6 1.0 copy-done.22
  456.6 1.0 copy-done.23
  460.4 10.4 %shard_map.280 = (bf16[4,384,768]{2,1,0:T(8,128)(2,1)}, bf16[4,768,1152]{2,1,0:T(8,128)(2,1)}, bf16[4,768,1536]{2,1,0:T(8,128)(2,1)}, bf16[4,1536,768]{2,1,0:T(8,128)(2,1)}) custom-call(bf16[4,384,768]{2,1,0:T(8,128)(2,1)S(1)} %copy-done.1, bf16[4,768,1152]{2,1,0:T(8,128)(2,1)S(1)} %copy-done, bf16[4,96,384]{2,1,0:T(8,128)(2,1)S(1)} %copy-done.23, ...), custom_call_target="tpu_custom_call" | custom-call | flops 12000000 | bytes 38000000 | tf_op jit(solution)/shard_map/pallas_call | solution.py:571
  470.8 1.9 constant_dynamic-update-slice_fusion.17
  472.7 1.9 constant_dynamic-update-slice_fusion.9
  475.3 1.9 constant_dynamic-update-slice_fusion.8
  477.2 1.4 collective-permute-start.14
  479.3 1.9 constant_dynamic-update-slice_fusion.7
  481.2 1.9 constant_dynamic-update-slice_fusion.6
  483.1 1.4 collective-permute-start.26
  484.5 1.9 constant_dynamic-update-slice_fusion.5
  487.2 34.7 %collective-permute-done.26 = bf16[1,192,768]{2,1,0:T(8,128)(2,1)S(1)} collective-permute-done((bf16[1,192,768]{2,1,0:T(8,128)(2,1)S(1)}, bf16[1,192,768]{2,1,0:T(8,128)(2,1)S(1)}, u32[]{:S(2)}, u32[]{:S(2)}) %collective-permute-start.26) | collective-permute-done | bytes 294944 | tf_op jit(solution)/shard_map/ppermute | solution.py:642
  (122 shorter events, 26.0 us)
Async XLA Ops:
  371.4 29.0 %collective-permute-start.1 = (bf16[1,192,1536]{2,1,0:T(8,128)(2,1)}, bf16[1,192,1536]{2,1,0:T(8,128)(2,1)S(1)}, u32[]{:S(2)}, u32[]{:S(2)}) collective-permute-start(bf16[1,192,1536]{2,1,0:T(8,128)(2,1)} %get-tuple-element.40.refs_4_), channel_id=1, source_target_pairs={{0,1},{1,0},{2,3},{3,2},{4,5},{5,4},{6,7},{7,6}} | collective-permute-start | bytes 1769480 | tf_op jit(solution)/shard_map/ppermute | solution.py:644
  371.5 29.6 %collective-permute-start.2 = (bf16[1,192,1536]{2,1,0:T(8,128)(2,1)}, bf16[1,192,1536]{2,1,0:T(8,128)(2,1)S(1)}, u32[]{:S(2)}, u32[]{:S(2)}) collective-permute-start(bf16[1,192,1536]{2,1,0:T(8,128)(2,1)} %get-tuple-element.41.refs_5_), channel_id=1, source_target_pairs={{0,1},{1,0},{2,3},{3,2},{4,5},{5,4},{6,7},{7,6}} | collective-permute-start | bytes 1769480 | tf_op jit(solution)/shard_map/ppermute | solution.py:644
  372.0 16.4 %collective-permute-start.8 = (bf16[1,192,768]{2,1,0:T(8,128)(2,1)}, bf16[1,192,768]{2,1,0:T(8,128)(2,1)S(1)}, u32[]{:S(2)}, u32[]{:S(2)}) collective-permute-start(bf16[1,192,768]{2,1,0:T(8,128)(2,1)} %get-tuple-element.47.refs_11_), channel_id=1, source_target_pairs={{0,1},{1,0},{2,3},{3,2},{4,5},{5,4},{6,7},{7,6}} | collective-permute-start | bytes 884744 | tf_op jit(solution)/shard_map/ppermute | solution.py:644
  372.0 17.6 %collective-permute-start.9 = (bf16[1,192,768]{2,1,0:T(8,128)(2,1)}, bf16[1,192,768]{2,1,0:T(8,128)(2,1)S(1)}, u32[]{:S(2)}, u32[]{:S(2)}) collective-permute-start(bf16[1,192,768]{2,1,0:T(8,128)(2,1)} %get-tuple-element.48.refs_12_), channel_id=1, source_target_pairs={{0,1},{1,0},{2,3},{3,2},{4,5},{5,4},{6,7},{7,6}} | collective-permute-start | bytes 884744 | tf_op jit(solution)/shard_map/ppermute | solution.py:644
  372.5 17.9 %collective-permute-start = (bf16[4,96,384]{2,1,0:T(8,128)(2,1)}, bf16[4,96,384]{2,1,0:T(8,128)(2,1)S(1)}, u32[]{:S(2)}, u32[]{:S(2)}) collective-permute-start(bf16[4,96,384]{2,1,0:T(8,128)(2,1)} %get-tuple-element.39.refs_2_), channel_id=1, source_target_pairs={{0,1},{1,0},{2,3},{3,2},{4,5},{5,4},{6,7},{7,6}} | collective-permute-start | bytes 884744 | tf_op jit(solution)/shard_map/ppermute | solution.py:643
  374.6 16.2 %copy-start.33 = (f32[4,192,1152]{2,1,0:T(8,128)S(1)}, f32[4,192,1152]{2,1,0:T(8,128)}, u32[]{:S(2)}) copy-start(f32[4,192,1152]{2,1,0:T(8,128)} %refs_5_.1) | copy-start | bytes 10616836
  389.1 12.0 %collective-permute-start.3 = (bf16[1,192,1536]{2,1,0:T(8,128)(2,1)S(1)}, bf16[1,192,1536]{2,1,0:T(8,128)(2,1)S(1)}, u32[]{:S(2)}, u32[]{:S(2)}) collective-permute-start(bf16[1,192,1536]{2,1,0:T(8,128)(2,1)S(1)} %copy-done.3), channel_id=1, source_target_pairs={{0,1},{1,0},{2,3},{3,2},{4,5},{5,4},{6,7},{7,6}} | collective-permute-start | bytes 1769480 | tf_op jit(solution)/shard_map/ppermute | solution.py:644
  390.3 13.0 %collective-permute-start.4 = (bf16[1,192,1536]{2,1,0:T(8,128)(2,1)S(1)}, bf16[1,192,1536]{2,1,0:T(8,128)(2,1)S(1)}, u32[]{:S(2)}, u32[]{:S(2)}) collective-permute-start(bf16[1,192,1536]{2,1,0:T(8,128)(2,1)S(1)} %copy-done.2), channel_id=1, source_target_pairs={{0,1},{1,0},{2,3},{3,2},{4,5},{5,4},{6,7},{7,6}} | collective-permute-start | bytes 1769480 | tf_op jit(solution)/shard_map/ppermute | solution.py:644
  390.4 14.5 %collective-permute-start.5 = (bf16[1,384,768]{2,1,0:T(8,128)(2,1)S(1)}, bf16[1,384,768]{2,1,0:T(8,128)(2,1)S(1)}, u32[]{:S(2)}, u32[]{:S(2)}) collective-permute-start(bf16[1,384,768]{2,1,0:T(8,128)(2,1)S(1)} %copy-done.5), channel_id=1, source_target_pairs={{0,1},{1,0},{2,3},{3,2},{4,5},{5,4},{6,7},{7,6}} | collective-permute-start | bytes 1769480 | tf_op jit(solution)/shard_map/ppermute | solution.py:644
  400.4 16.4 %collective-permute-start.18 = (bf16[1,384,768]{2,1,0:T(8,128)(2,1)S(1)}, bf16[1,384,768]{2,1,0:T(8,128)(2,1)}, u32[]{:S(2)}, u32[]{:S(2)}) collective-permute-start(bf16[1,384,768]{2,1,0:T(8,128)(2,1)S(1)} %copy-done.5), channel_id=1, source_target_pairs={{0,2},{1,3},{2,0},{3,1},{4,6},{5,7},{6,4},{7,5}} | collective-permute-start | bytes 1769480 | tf_op jit(solution)/shard_map/ppermute | solution.py:642
  401.1 13.5 %collective-permute-start.6 = (bf16[1,384,768]{2,1,0:T(8,128)(2,1)S(1)}, bf16[1,384,768]{2,1,0:T(8,128)(2,1)S(1)}, u32[]{:S(2)}, u32[]{:S(2)}) collective-permute-start(bf16[1,384,768]{2,1,0:T(8,128)(2,1)S(1)} %copy-done.7), channel_id=1, source_target_pairs={{0,1},{1,0},{2,3},{3,2},{4,5},{5,4},{6,7},{7,6}} | collective-permute-start | bytes 1769480 | tf_op jit(solution)/shard_map/ppermute | solution.py:644
  402.0 27.4 %collective-permute-start.20 = (bf16[1,384,768]{2,1,0:T(8,128)(2,1)S(1)}, bf16[1,384,768]{2,1,0:T(8,128)(2,1)}, u32[]{:S(2)}, u32[]{:S(2)}) collective-permute-start(bf16[1,384,768]{2,1,0:T(8,128)(2,1)S(1)} %copy-done.7), channel_id=1, source_target_pairs={{0,2},{1,3},{2,0},{3,1},{4,6},{5,7},{6,4},{7,5}} | collective-permute-start | bytes 1769480 | tf_op jit(solution)/shard_map/ppermute | solution.py:642
  404.1 37.9 %collective-permute-start.10 = (bf16[1,192,1536]{2,1,0:T(8,128)(2,1)}, bf16[1,192,1536]{2,1,0:T(8,128)(2,1)}, u32[]{:S(2)}, u32[]{:S(2)}) collective-permute-start(bf16[1,192,1536]{2,1,0:T(8,128)(2,1)} %get-tuple-element.40.refs_4_), channel_id=1, source_target_pairs={{0,2},{1,3},{2,0},{3,1},{4,6},{5,7},{6,4},{7,5}} | collective-permute-start | bytes 1769480 | tf_op jit(solution)/shard_map/ppermute | solution.py:642
  405.6 28.4 %collective-permute-start.7 = (bf16[1,384,768]{2,1,0:T(8,128)(2,1)}, bf16[1,384,768]{2,1,0:T(8,128)(2,1)}, u32[]{:S(2)}, u32[]{:S(2)}) collective-permute-start(bf16[1,384,768]{2,1,0:T(8,128)(2,1)} %get-tuple-element.46.refs_10_), channel_id=1, source_target_pairs={{0,1},{1,0},{2,3},{3,2},{4,5},{5,4},{6,7},{7,6}} | collective-permute-start | bytes 1769480 | tf_op jit(solution)/shard_map/ppermute | solution.py:644
  405.7 23.7 %copy-start.34 = (f32[4,96,768]{2,1,0:T(8,128)S(1)}, f32[4,96,768]{2,1,0:T(8,128)}, u32[]{:S(2)}) copy-start(f32[4,96,768]{2,1,0:T(8,128)} %refs_4_.1) | copy-start | bytes 3538948
  405.7 23.7 %copy-start.35 = (f32[4,96,768]{2,1,0:T(8,128)S(1)}, f32[4,96,768]{2,1,0:T(8,128)}, u32[]{:S(2)}) copy-start(f32[4,96,768]{2,1,0:T(8,128)} %refs_8_.1) | copy-start | bytes 3538948
  414.6 27.4 %copy-start.1 = (bf16[4,384,768]{2,1,0:T(8,128)(2,1)S(1)}, bf16[4,384,768]{2,1,0:T(8,128)(2,1)}, u32[]{:S(2)}) copy-start(bf16[4,384,768]{2,1,0:T(8,128)(2,1)} %get-tuple-element.37.refs_0_) | copy-start | bytes 7077892
  415.4 63.2 %collective-permute-start.22 = (bf16[1,384,768]{2,1,0:T(8,128)(2,1)}, bf16[1,384,768]{2,1,0:T(8,128)(2,1)}, u32[]{:S(2)}, u32[]{:S(2)}) collective-permute-start(bf16[1,384,768]{2,1,0:T(8,128)(2,1)} %get-tuple-element.46.refs_10_), channel_id=1, source_target_pairs={{0,2},{1,3},{2,0},{3,1},{4,6},{5,7},{6,4},{7,5}} | collective-permute-start | bytes 1769480 | tf_op jit(solution)/shard_map/ppermute | solution.py:642
  416.8 57.8 %collective-permute-start.19 = (bf16[1,384,768]{2,1,0:T(8,128)(2,1)}, bf16[1,384,768]{2,1,0:T(8,128)(2,1)}, u32[]{:S(2)}, u32[]{:S(2)}) collective-permute-start(bf16[1,384,768]{2,1,0:T(8,128)(2,1)} %collective-permute-done.18), channel_id=1, source_target_pairs={{0,1},{1,0},{2,3},{3,2},{4,5},{5,4},{6,7},{7,6}} | collective-permute-start | bytes 1769480 | tf_op jit(solution)/shard_map/ppermute | solution.py:647
  429.4 49.9 %collective-permute-start.21 = (bf16[1,384,768]{2,1,0:T(8,128)(2,1)}, bf16[1,384,768]{2,1,0:T(8,128)(2,1)}, u32[]{:S(2)}, u32[]{:S(2)}) collective-permute-start(bf16[1,384,768]{2,1,0:T(8,128)(2,1)} %collective-permute-done.20), channel_id=1, source_target_pairs={{0,1},{1,0},{2,3},{3,2},{4,5},{5,4},{6,7},{7,6}} | collective-permute-start | bytes 1769480 | tf_op jit(solution)/shard_map/ppermute | solution.py:647
  434.1 43.1 %collective-permute-start.24 = (bf16[1,192,768]{2,1,0:T(8,128)(2,1)}, bf16[1,192,768]{2,1,0:T(8,128)(2,1)S(1)}, u32[]{:S(2)}, u32[]{:S(2)}) collective-permute-start(bf16[1,192,768]{2,1,0:T(8,128)(2,1)} %get-tuple-element.47.refs_11_), channel_id=1, source_target_pairs={{0,2},{1,3},{2,0},{3,1},{4,6},{5,7},{6,4},{7,5}} | collective-permute-start | bytes 884744 | tf_op jit(solution)/shard_map/ppermute | solution.py:642
  442.0 41.1 %collective-permute-start.11 = (bf16[1,192,1536]{2,1,0:T(8,128)(2,1)}, bf16[1,192,1536]{2,1,0:T(8,128)(2,1)S(1)}, u32[]{:S(2)}, u32[]{:S(2)}) collective-permute-start(bf16[1,192,1536]{2,1,0:T(8,128)(2,1)} %collective-permute-done.10), channel_id=1, source_target_pairs={{0,1},{1,0},{2,3},{3,2},{4,5},{5,4},{6,7},{7,6}} | collective-permute-start | bytes 1769480 | tf_op jit(solution)/shard_map/ppermute | solution.py:647
  474.6 47.3 %collective-permute-start.12 = (bf16[1,192,1536]{2,1,0:T(8,128)(2,1)S(1)}, bf16[1,192,1536]{2,1,0:T(8,128)(2,1)S(1)}, u32[]{:S(2)}, u32[]{:S(2)}) collective-permute-start(bf16[1,192,1536]{2,1,0:T(8,128)(2,1)S(1)} %copy-done.4), channel_id=1, source_target_pairs={{0,2},{1,3},{2,0},{3,1},{4,6},{5,7},{6,4},{7,5}} | collective-permute-start | bytes 1769480 | tf_op jit(solution)/shard_map/ppermute | solution.py:642
  477.2 45.3 %collective-permute-start.14 = (bf16[1,192,1536]{2,1,0:T(8,128)(2,1)S(1)}, bf16[1,192,1536]{2,1,0:T(8,128)(2,1)S(1)}, u32[]{:S(2)}, u32[]{:S(2)}) collective-permute-start(bf16[1,192,1536]{2,1,0:T(8,128)(2,1)S(1)} %copy-done.3), channel_id=1, source_target_pairs={{0,2},{1,3},{2,0},{3,1},{4,6},{5,7},{6,4},{7,5}} | collective-permute-start | bytes 1769480 | tf_op jit(solution)/shard_map/ppermute | solution.py:642
  478.6 43.9 %collective-permute-start.16 = (bf16[1,192,1536]{2,1,0:T(8,128)(2,1)S(1)}, bf16[1,192,1536]{2,1,0:T(8,128)(2,1)S(1)}, u32[]{:S(2)}, u32[]{:S(2)}) collective-permute-start(bf16[1,192,1536]{2,1,0:T(8,128)(2,1)S(1)} %copy-done.2), channel_id=1, source_target_pairs={{0,2},{1,3},{2,0},{3,1},{4,6},{5,7},{6,4},{7,5}} | collective-permute-start | bytes 1769480 | tf_op jit(solution)/shard_map/ppermute | solution.py:642
  479.2 43.8 %collective-permute-start.23 = (bf16[1,384,768]{2,1,0:T(8,128)(2,1)}, bf16[1,384,768]{2,1,0:T(8,128)(2,1)S(1)}, u32[]{:S(2)}, u32[]{:S(2)}) collective-permute-start(bf16[1,384,768]{2,1,0:T(8,128)(2,1)} %collective-permute-done.22), channel_id=1, source_target_pairs={{0,1},{1,0},{2,3},{3,2},{4,5},{5,4},{6,7},{7,6}} | collective-permute-start | bytes 1769480 | tf_op jit(solution)/shard_map/ppermute | solution.py:647
  483.1 38.9 %collective-permute-start.26 = (bf16[1,192,768]{2,1,0:T(8,128)(2,1)S(1)}, bf16[1,192,768]{2,1,0:T(8,128)(2,1)S(1)}, u32[]{:S(2)}, u32[]{:S(2)}) collective-permute-start(bf16[1,192,768]{2,1,0:T(8,128)(2,1)S(1)} %copy-done.21), channel_id=1, source_target_pairs={{0,2},{1,3},{2,0},{3,1},{4,6},{5,7},{6,4},{7,5}} | collective-permute-start | bytes 884744 | tf_op jit(solution)/shard_map/ppermute | solution.py:642
  522.0 3.5 collective-permute-start.25
  522.0 9.2 %collective-permute-start.27 = (bf16[1,192,768]{2,1,0:T(8,128)(2,1)S(1)}, bf16[1,192,768]{2,1,0:T(8,128)(2,1)S(1)}, u32[]{:S(2)}, u32[]{:S(2)}) collective-permute-start(bf16[1,192,768]{2,1,0:T(8,128)(2,1)S(1)} %collective-permute-done.26), channel_id=1, source_target_pairs={{0,1},{1,0},{2,3},{3,2},{4,5},{5,4},{6,7},{7,6}} | collective-permute-start | bytes 884744 | tf_op jit(solution)/shard_map/ppermute | solution.py:647
  522.5 3.7 collective-permute-start.13
  522.5 5.4 %collective-permute-start.15 = (bf16[1,192,1536]{2,1,0:T(8,128)(2,1)S(1)}, bf16[1,192,1536]{2,1,0:T(8,128)(2,1)S(1)}, u32[]{:S(2)}, u32[]{:S(2)}) collective-permute-start(bf16[1,192,1536]{2,1,0:T(8,128)(2,1)S(1)} %collective-permute-done.14), channel_id=1, source_target_pairs={{0,1},{1,0},{2,3},{3,2},{4,5},{5,4},{6,7},{7,6}} | collective-permute-start | bytes 1769480 | tf_op jit(solution)/shard_map/ppermute | solution.py:647
  523.0 7.4 %collective-permute-start.17 = (bf16[1,192,1536]{2,1,0:T(8,128)(2,1)S(1)}, bf16[1,192,1536]{2,1,0:T(8,128)(2,1)S(1)}, u32[]{:S(2)}, u32[]{:S(2)}) collective-permute-start(bf16[1,192,1536]{2,1,0:T(8,128)(2,1)S(1)} %collective-permute-done.16), channel_id=1, source_target_pairs={{0,1},{1,0},{2,3},{3,2},{4,5},{5,4},{6,7},{7,6}} | collective-permute-start | bytes 1769480 | tf_op jit(solution)/shard_map/ppermute | solution.py:647
  (32 other events, 161.3 us)

commit v2 on v1

--- a/solution.py
+++ b/solution.py
@@ -43,7 +43,9 @@
 SENT_GROUPS = SENT_UNITS // PAIR
 PIECE_UNITS = FIRST[FCOUT] - FIRST[FCIN]
 LATE_GROUPS = 2
-RELAYED = SENT_GROUPS - LATE_GROUPS
+TAIL_GROUPS = 5
+TAIL_FIRST = SENT_GROUPS - TAIL_GROUPS
+RELAYED = TAIL_FIRST - LATE_GROUPS
 LAST_ROWS = 192
 PIECES = tuple(
     [(layer, 0, SHARD_ROWS[kind]) for layer in range(LAYERS - (kind == FCOUT))]
@@ -114,12 +116,13 @@
 
 def step_kernel(*refs):
     counts = tuple(map(len, PIECES))
-    grads, weights, firsts, seconds, means, reps, in_pieces, out_pieces, rest = split(refs, *[len(KINDS)] * 5, PAIR, *counts, 20)
+    grads, weights, firsts, seconds, means, reps, in_pieces, out_pieces, rest = split(refs, *[len(KINDS)] * 5, PAIR, *counts, 22)
     pieces = {FCIN: in_pieces, FCOUT: out_pieces}
-    (late, scal_out, recv, stage, mean, held, ring, note, notes, w_sums, u_sums, n_sum, scal,
+    (late, tail, extra, scal_out, recv, stage, mean, held, ring, note, notes, w_sums, u_sums, n_sum, scal,
      ring_sem, held_sem, mean_sem, send_sem, recv_sem, rep_send_sem, note_sem) = rest
     model, data = lax.axis_index("model"), lax.axis_index("data")
     partner = partners(data)
+    stays = data % PAIR == 1
 
     def unit_at(ref, kind, index, quarter_base=None):
         layer, row, col = place(kind, index)
@@ -400,25 +403,27 @@
         return remote(source, recv.at[k - 1, pair(group)], rep_send_sem.at[k - 1], recv_sem.at[arrival], FAR if k == FAR else NEAR)
 
     def late_copy(group):
-        return remote(stage.at[pair(group)], late.at[pair(group - RELAYED)], rep_send_sem.at[FAR - 1], recv_sem.at[group], FAR)
+        target = late.at[pair(group - RELAYED)] if group < TAIL_FIRST else tail.at[pair(group - TAIL_FIRST)]
+        return remote(stage.at[pair(group)], target, rep_send_sem.at[FAR - 1], recv_sem.at[group], FAR)
 
     def all_copies(k, count):
         return remote(landed(count), landed(count), rep_send_sem.at[k - 1], recv_sem.at[near_sem], NEAR)
 
     def start_replicas(unit_from, unit_to):
         def body(group, _):
-            @pl.when(group < RELAYED)
-            def _():
-                rep_copy(group, FAR).start()
-
-            @pl.when(group >= RELAYED)
-            def _():
-                late_copy(group).start()
-
+            rep_copy(group, FAR).start()
             rep_copy(group, NEAR).start()
             return 0
 
         lax.fori_loop(unit_from // PAIR, unit_to // PAIR, body, 0)
+
+    def start_late_replicas():
+        for group in range(RELAYED, SENT_GROUPS):
+            if group < TAIL_FIRST:
+                late_copy(group).start()
+            else:
+                pl.when(stays)(late_copy(group).start)
+            rep_copy(group, NEAR).start()
 
     def replicas_out(unit_from, unit_to, k):
         def unit_step(unit, _):
@@ -466,17 +471,20 @@
     ratios(QKV)
     new_weights(QKV, 0, half, stage)
     directions(FCIN, piece_end // PAIR, piece_end // PAIR + PAIR)
-    start_replicas(proj_end, proj_end + half)
+    start_replicas(proj_end, proj_end + half // PAIR)
     directions(FCIN, piece_end // PAIR + PAIR, piece_end)
     refill(FIRST[FCIN], FIRST[FCOUT])
     new_weights(QKV, half, qkv_end, stage)
     directions(FCOUT, 0, piece_end)
     write_note(FCIN)
     write_note(FCOUT)
-    replicas_out(0, SENT_UNITS, OWN)
+    extra_copy = pltpu.make_async_copy(stage.at[pl.ds(PAIR * TAIL_FIRST, PAIR * TAIL_GROUPS)], extra, mean_sem.at[SEND_SLOTS - 1])
+    extra_copy.start()
     send_note(FCIN)
     send_note(FCOUT)
-    start_replicas(proj_end + half, SENT_UNITS)
+    start_replicas(proj_end + half // PAIR, PAIR * RELAYED)
+    start_late_replicas()
+    replicas_out(0, SENT_UNITS, OWN)
     for kind in (FCIN, FCOUT):
         ratios(kind)
         new_weights(kind, 0, piece_end, recv.at[0])
@@ -484,6 +492,8 @@
     scal_copy.start()
     pieces_out(FCIN)
     pieces_out(FCOUT)
+    all_copies(NEAR, SENT_UNITS).wait()
+    replicas_out(0, SENT_UNITS, NEAR)
 
     def relay_step(group, _):
         @pl.when(group < RELAYED)
@@ -500,15 +510,23 @@
         return 0
 
     lax.fori_loop(0, RELAYED + 1, relay_step, 0)
-    all_copies(NEAR, SENT_UNITS).wait()
-    replicas_out(0, SENT_UNITS, NEAR)
-    all_copies(FAR, SENT_UNITS).wait_send()
     all_copies(CROSS, PAIR * RELAYED).wait_send()
     for index, count in enumerate((SENT_UNITS, SENT_UNITS, PAIR * RELAYED, PAIR * RELAYED, PIECE_UNITS, PIECE_UNITS)):
         pltpu.make_async_copy(landed(count), landed(count), mean_sem.at[index]).wait()
     scal_copy.wait()
-    for group in range(RELAYED, SENT_GROUPS):
+    extra_copy.wait()
+    for group in range(RELAYED, TAIL_FIRST):
         late_copy(group).wait_recv()
+
+    @pl.when(stays)
+    def _():
+        all_copies(FAR, SENT_UNITS).wait_send()
+        for group in range(TAIL_FIRST, SENT_GROUPS):
+            late_copy(group).wait_recv()
+
+    @pl.when(jnp.logical_not(stays))
+    def _():
+        all_copies(FAR, PAIR * TAIL_FIRST).wait_send()
 
 
 def place_static(kind, index):
@@ -525,7 +543,7 @@
 
 
 def assemble_kernel(*refs):
-    (proj, qkv, late, late_near), own, near, outs, scratch = split(refs, len(KINDS), PIECE_COUNT, PIECE_COUNT, len(KINDS), 7)
+    (proj, qkv), far_parts, cross_parts, own, near, outs, scratch = split(refs, PAIR, PAIR, PAIR, PIECE_COUNT, PIECE_COUNT, len(KINDS), 7)
     proj_buf, qkv_buf, in_buf, out_buf, late_sem, whole_sem, piece_sem = scratch
     partner = partners(lax.axis_index("data"))
     copies = []
@@ -542,32 +560,36 @@
             at = (in_buf if kind == FCIN else out_buf).at[k, pl.ds(layer, 1), pl.ds(first, rows)]
             base = pl.multiple_of(partner[k] * SHARD_ROWS[kind] + first, UNIT_ROWS)
             through(piece, at, outs[kind].at[pl.ds(layer, 1), pl.ds(base, rows)], piece_sem.at[k, number])
+    fills = [[] for _ in range(LAYERS)]
+    for k, sources in ((FAR, far_parts), (CROSS, cross_parts)):
+        units = [source.at[unit] for source in sources for unit in range(source.shape[0])]
+        for number, source in enumerate(units):
+            layer, row, col = place_static(QKV, PAIR * RELAYED + number - FIRST[QKV])
+            base = pl.multiple_of(partner[k] * SHARD_ROWS[QKV] + row, UNIT_ROWS)
+            target = qkv_buf.at[layer, pl.ds(base, UNIT_ROWS), pl.ds(col, UNIT_COLS)]
+            fills[layer].append(pltpu.make_async_copy(source, target, late_sem.at[k - FAR, number]))
     for fetch, _ in copies:
         fetch.start()
-    for position, (fetch, store) in enumerate(copies):
+    for (fetch, _), layer_fills in zip(copies, fills):
         fetch.wait()
-        if position == LAYERS - 1:
-            fills = []
-            for k, source in ((FAR, late), (CROSS, late_near)):
-                for unit in range(PAIR * LATE_GROUPS):
-                    layer, row, col = place_static(QKV, PAIR * RELAYED + unit - FIRST[QKV])
-                    base = pl.multiple_of(partner[k] * SHARD_ROWS[QKV] + row, UNIT_ROWS)
-                    target = qkv_buf.at[layer, pl.ds(base, UNIT_ROWS), pl.ds(col, UNIT_COLS)]
-                    fills.append(pltpu.make_async_copy(source.at[unit], target, late_sem.at[k - FAR, unit]))
-            for fill in fills:
-                fill.start()
-            for fill in fills:
-                fill.wait()
+        for fill in layer_fills:
+            fill.start()
+    for (_, store), layer_fills in zip(copies, fills):
+        for fill in layer_fills:
+            fill.wait()
+        store.start()
+    for fetch, store in copies[LAYERS:]:
+        fetch.wait()
         store.start()
     for _, store in copies:
         store.wait()
 
 
-def assemble(reps, late, late_near, own, near):
+def assemble(reps, far_parts, cross_parts, own, near):
     shape, dma = jax.ShapeDtypeStruct, pltpu.SemaphoreType.DMA
     whole = [(LAYERS, len(PARTNERS) * rows, cols) for rows, cols in zip(SHARD_ROWS, SHARD_COLS)]
     any_spec = pl.BlockSpec(memory_space=pl.ANY)
-    operands = [*reps, late, late_near, *own, *near]
+    operands = [*reps, *far_parts, *cross_parts, *own, *near]
     return pl.pallas_call(
         assemble_kernel,
         out_shape=[shape(s, BF16) for s in whole],
@@ -578,7 +600,7 @@
             pltpu.VMEM(whole[QKV], BF16),
             pltpu.VMEM((PAIR, LAYERS, SHARD_ROWS[FCIN], SHARD_COLS[FCIN]), BF16),
             pltpu.VMEM((PAIR, LAYERS, SHARD_ROWS[FCOUT], SHARD_COLS[FCOUT]), BF16),
-            dma((PAIR, PAIR * LATE_GROUPS)), dma((LAYERS + 1, PAIR)), dma((PAIR, len(own), PAIR)),
+            dma((PAIR, SENT_UNITS - PAIR * RELAYED)), dma((LAYERS + 1, PAIR)), dma((PAIR, len(own), PAIR)),
         ],
         compiler_params=pltpu.CompilerParams(vmem_limit_bytes=24_000_000),
         cost_estimate=pl.CostEstimate(flops=12_000_000, bytes_accessed=38_000_000, transcendentals=0),
@@ -591,20 +613,21 @@
         in_specs.extend([grad_spec(col_split), state_spec(col_split), state_spec(col_split), state_spec(col_split)])
     out_specs = tuple([replica_spec(col_split) for col_split in COLUMN_SPLIT] + [state_spec(col_split) for col_split in COLUMN_SPLIT] * 3)
     across, beside = ([(i, partners(i)[k]) for i in PARTNERS] for k in (FAR, NEAR))
+    leavers = [(i, k) for i, k in across if i % PAIR == 0]
 
     def device_step(*arrays):
         shape = jax.ShapeDtypeStruct
         shard = [(LAYERS, rows, cols) for rows, cols in zip(SHARD_ROWS, SHARD_COLS)]
         order = [(kind, piece) for kind in (FCIN, FCOUT) for piece in PIECES[kind - FCIN]]
         scal_shape = (len(KINDS) + 1,) + TILE
+        unit = (UNIT_ROWS, UNIT_COLS)
         out_shape = (
             [shape(s, F32) for s in shard]
             + [shape((LAYERS, len(PARTNERS) * SHARD_ROWS[kind], SHARD_COLS[kind]), BF16) for kind in (PROJ, QKV)]
             + [shape((1, rows, SHARD_COLS[kind]), BF16) for kind, (_, _, rows) in order]
-            + [shape((PAIR * LATE_GROUPS, UNIT_ROWS, UNIT_COLS), BF16), shape(scal_shape, F32)])
+            + [shape((PAIR * count,) + unit, BF16) for count in (LATE_GROUPS, TAIL_GROUPS, TAIL_GROUPS)] + [shape(scal_shape, F32)])
         any_spec = pl.BlockSpec(memory_space=pl.ANY)
         dma = pltpu.SemaphoreType.DMA
-        unit = (UNIT_ROWS, UNIT_COLS)
         messages = len(KINDS) + PAIR
         operands = [arrays[len(KINDS) * kind + part] for part in PARTNERS for kind in KIND_ORDER]
         results = pl.pallas_call(
@@ -628,8 +651,9 @@
             ],
             compiler_params=pltpu.CompilerParams(collective_id=0, has_side_effects=True, vmem_limit_bytes=66_900_000),
         )(*operands)
-        means, reps, pieces, (late, scal) = split(results, len(KINDS), PAIR, PIECE_COUNT, PAIR)
-        owners = partners(lax.axis_index("data"))
+        means, reps, pieces, (late, tail, extra, scal) = split(results, len(KINDS), PAIR, PIECE_COUNT, 4)
+        data = lax.axis_index("data")
+        owners = partners(data)
         state = {}
         clip = scal[len(KINDS), 0, 0]
         for slot, kind in enumerate(KIND_ORDER):
@@ -640,9 +664,11 @@
         far, near = [], []
         for piece in pieces:
             far.append(lax.ppermute(piece, "data", across))
-        late_near = lax.ppermute(late, "data", beside)
+        arrived = lax.ppermute(extra, "data", leavers)
+        far_parts = (late, jnp.where(data % PAIR == 0, arrived, tail))
+        cross_parts = [lax.ppermute(part, "data", beside) for part in far_parts]
         near = [lax.ppermute(piece, "data", beside) for piece in pieces]
-        replicas = list(assemble(reps, late, late_near, pieces, near))
+        replicas = list(assemble(reps, far_parts, cross_parts, pieces, near))
         for number, (kind, (layer, first, _)) in enumerate(order):
             far_near = lax.ppermute(far[number], "data", beside)
             for piece, k in ((far[number], FAR), (far_near, CROSS)):

time: 533 us -> 508 us (0.953)
  waiting for transfers between devices: 54.5 us -> 37.1 us
  Pallas kernels: 381 us -> 366 us
  starting transfers between devices: 12.1 us -> 22.8 us
    ppermute x9, waiting for transfers between devices: 54.4 us -> 37 us  [device_step(): far.append(lax.ppermute(piece, 'data', across))]
    pallas_call x1, Pallas kernels: 371 us -> 356 us  [device_step(): pl.pallas_call(step_kernel, out_shape=out_shape, in_specs=[any_spec] * le...]
    ppermute x9, starting transfers between devices: 2.06 us -> 8.5 us  [device_step(): near = [lax.ppermute(piece, 'data', beside) for piece in pieces]]
    unnamed x72 -> x70, local copies, waits for them, and re-layouts: 23.1 us -> 19.4 us
  transfers between devices with their start and end apart: 28 -> 30, of which waited for: 3 -> 2; matrix products, arithmetic and copies ran while one was open for 11% -> 12% of each run, Pallas kernels for 2% -> 2%
where the time goes in v2:
time: 508 us; the launch traced here: 507 us
  Pallas kernels  366 us (72%)
  local copies, waits for them, and re-layouts  41.9 us (8%)
  other arithmetic  38.6 us (8%)
  waiting for transfers between devices  37.1 us (7%)
  starting transfers between devices  22.8 us (4%)
    pallas_call x1, Pallas kernels, device_step(): pl.pallas_call(step_kernel, out_shape=out_shape, in_specs=[any_spec] * le...  356 us
    ppermute x9, waiting for transfers between devices, device_step(): far.append(lax.ppermute(piece, 'data', across))  37 us
    sub x4, other arithmetic, device_step(): state[kind] = (weight - LEARN_RATE * ratio * update, new_first, new_second)  36.5 us
    dynamic_update_slice x18, local copies, waits for them, and re-layouts, device_step(): lax.dynamic_update_slice(replicas[kind], piece, (layer, owners[k] * SHARD...  21.3 us
    unnamed x70, local copies, waits for them, and re-layouts  19.4 us
    pallas_call x1, Pallas kernels, assemble(): pl.pallas_call(assemble_kernel, out_shape=[shape(s, BF16) for s in whole]...  10.4 us
  transfers between devices with their start and end apart: 30, of which 2 were waited for; matrix products, arithmetic and copies ran while one was open for 12% of the time, Pallas kernels for 2%

profile of v2, /device:TPU:0, one launch (start us, length us, event | category | flops | bytes accessed | tf_op | source)
XLA Modules:
  0.0 507.2 jit_solution(3706857155834410856)
XLA Ops:
  0.6 355.6 %shard_map.279 = (f32[4,96,768]{2,1,0:T(8,128)}, f32[4,192,1152]{2,1,0:T(8,128)}, f32[4,192,1536]{2,1,0:T(8,128)}, f32[4,384,768]{2,1,0:T(8,128)}, bf16[4,384,76...) custom-call(f32[1,4,384,768]{3,2,1,0:T(8,128)} %refs_0_.1, ...), custom_call_target="tpu_custom_call" | custom-call | tf_op jit(solution)/shard_map/pallas_call | solution.py:633
  356.2 7.2 %collective-permute-start.10 = (bf16[1,192,768]{2,1,0:T(8,128)(2,1)}, bf16[1,192,768]{2,1,0:T(8,128)(2,1)S(1)}, u32[]{:S(2)}, u32[]{:S(2)}) collective-permute-start(bf16[1,192,768]{2,1,0:T(8,128)(2,1)} %get-tuple-element.51.refs_13_), channel_id=1, source_target_pairs={{0,1},{1,0},{2,3},{3,2},{4,5},{5,4},{6,7},{7,6}} | collective-permute-start | bytes 884744 | tf_op jit(solution)/shard_map/ppermute | solution.py:670
  363.4 2.7 collective-permute-start
  366.7 1.2 slice.16
  370.0 14.0 %multiply_subtract_fusion.1 = (f32[4,192,1536]{2,1,0:T(8,128)}, f32[4,192,1536]{2,1,0:T(8,128)}, f32[4,192,1536]{2,1,0:T(8,128)}) fusion(f32[4,192,1536]{2,1,0:T(8,128)} %refs_6_.1, f32[4]{0:T(128)S(1)} %get-tuple-element.63, f32[4,192,1536]{2,1,0:T(8,128)} %get-tuple-element.60, f32[]{:T(128)} %bitcast, f32[4,192,1536]{2,1,0:T(8,128)} %refs_10_.1, ...), kind=kLoop, calls=%fused_computation.7 | loop fusion | flops 18874368 | bytes 33030164 | tf_op jit(solution)/shard_map/sub | solution.py:663
  384.7 1.4 collective-permute-start.20
  386.8 5.6 %multiply_subtract_fusion.2 = (f32[4,192,1152]{2,1,0:T(8,128)}, f32[4,192,1152]{2,1,0:T(8,128)}, f32[4,192,1152]{2,1,0:T(8,128)}) fusion(f32[4,192,1152]{2,1,0:T(8,128)S(1)} %copy-done.26, f32[4]{0:T(128)S(1)} %get-tuple-element.65, f32[4,192,1152]{2,1,0:T(8,128)S(1)} %copy-done.32, f32[]{:T(128)} %bitcast, f32[4,192,1152]{2,1,0:T(8,128)S(1)} %copy-done.27, ...), kind=kLoop, calls=%fused_computation.10 | loop fusion | flops 14155776 | bytes 24772628 | tf_op jit(solution)/shard_map/sub | solution.py:663
  392.4 1.2 broadcast_select_fusion.refs_3_
  394.6 1.2 collective-permute-start.12
  396.5 4.5 collective-permute-done.20
  401.5 14.0 %multiply_subtract_fusion = (f32[4,384,768]{2,1,0:T(8,128)}, f32[4,384,768]{2,1,0:T(8,128)}, f32[4,384,768]{2,1,0:T(8,128)}) fusion(f32[4,384,768]{2,1,0:T(8,128)} %refs_7_.1, f32[4]{0:T(128)S(1)} %get-tuple-element.62, f32[4,384,768]{2,1,0:T(8,128)} %get-tuple-element.61, f32[]{:T(128)} %bitcast, f32[4,384,768]{2,1,0:T(8,128)} %refs_11_.1, ...), kind=kLoop, calls=%fused_computation.5 | loop fusion | flops 18874368 | bytes 33030164 | tf_op jit(solution)/shard_map/sub | solution.py:663
  416.4 1.4 collective-permute-start.24
  417.8 3.0 multiply_subtract_fusion.3
  421.5 3.0 copy-done
  424.5 1.1 copy-done.3
  425.5 1.1 copy-done.5
  426.6 1.1 copy-done.6
  427.7 1.1 copy-done.8
  428.7 1.1 copy-done.10
  429.8 1.1 copy-done.12
  430.9 1.1 copy-done.14
  431.9 1.1 copy-done.16
  437.8 10.4 %shard_map.280 = (bf16[4,384,768]{2,1,0:T(8,128)(2,1)}, bf16[4,768,1152]{2,1,0:T(8,128)(2,1)}, bf16[4,768,1536]{2,1,0:T(8,128)(2,1)}, bf16[4,1536,768]{2,1,0:T(8,128)(2,1)}) custom-call(bf16[4,384,768]{2,1,0:T(8,128)(2,1)S(1)} %copy-done.1, bf16[4,768,1152]{2,1,0:T(8,128)(2,1)S(1)} %copy-done, bf16[4,96,384]{2,1,0:T(8,128)(2,1)S(1)} %copy-done.19, ...), custom_call_target="tpu_custom_call" | custom-call | flops 12000000 | bytes 38000000 | tf_op jit(solution)/shard_map/pallas_call | solution.py:593
  448.2 1.9 constant_dynamic-update-slice_fusion.9
  450.2 1.4 collective-permute-start.14
  451.5 1.9 constant_dynamic-update-slice_fusion.8
  453.4 1.9 constant_dynamic-update-slice_fusion.7
  456.0 1.9 constant_dynamic-update-slice_fusion.6
  457.9 1.4 collective-permute-start.18
  459.3 1.9 constant_dynamic-update-slice_fusion.17
  461.9 1.9 constant_dynamic-update-slice_fusion.5
  464.7 32.5 %collective-permute-done.28 = bf16[1,192,768]{2,1,0:T(8,128)(2,1)S(1)} collective-permute-done((bf16[1,192,768]{2,1,0:T(8,128)(2,1)S(1)}, bf16[1,192,768]{2,1,0:T(8,128)(2,1)S(1)}, u32[]{:S(2)}, u32[]{:S(2)}) %collective-permute-start.28) | collective-permute-done | bytes 294944 | tf_op jit(solution)/shard_map/ppermute | solution.py:666
  (125 shorter events, 24.8 us)
Async XLA Ops:
  356.2 12.5 %collective-permute-start.10 = (bf16[1,192,768]{2,1,0:T(8,128)(2,1)}, bf16[1,192,768]{2,1,0:T(8,128)(2,1)S(1)}, u32[]{:S(2)}, u32[]{:S(2)}) collective-permute-start(bf16[1,192,768]{2,1,0:T(8,128)(2,1)} %get-tuple-element.51.refs_13_), channel_id=1, source_target_pairs={{0,1},{1,0},{2,3},{3,2},{4,5},{5,4},{6,7},{7,6}} | collective-permute-start | bytes 884744 | tf_op jit(solution)/shard_map/ppermute | solution.py:670
  363.4 23.3 %collective-permute-start = (bf16[10,96,384]{2,1,0:T(8,128)(2,1)}, bf16[10,96,384]{2,1,0:T(8,128)(2,1)S(1)}, u32[]{:S(2)}, u32[]{:S(2)}) collective-permute-start(bf16[10,96,384]{2,1,0:T(8,128)(2,1)} %get-tuple-element.42), channel_id=1, source_target_pairs={{0,2},{2,0},{4,6},{6,4}} | collective-permute-start | bytes 2211848 | tf_op jit(solution)/shard_map/ppermute | solution.py:667
  366.1 19.9 %collective-permute-start.3 = (bf16[1,192,1536]{2,1,0:T(8,128)(2,1)}, bf16[1,192,1536]{2,1,0:T(8,128)(2,1)S(1)}, u32[]{:S(2)}, u32[]{:S(2)}) collective-permute-start(bf16[1,192,1536]{2,1,0:T(8,128)(2,1)} %get-tuple-element.44.refs_6_), channel_id=1, source_target_pairs={{0,1},{1,0},{2,3},{3,2},{4,5},{5,4},{6,7},{7,6}} | collective-permute-start | bytes 1769480 | tf_op jit(solution)/shard_map/ppermute | solution.py:670
  366.2 20.1 %collective-permute-start.4 = (bf16[1,192,1536]{2,1,0:T(8,128)(2,1)}, bf16[1,192,1536]{2,1,0:T(8,128)(2,1)S(1)}, u32[]{:S(2)}, u32[]{:S(2)}) collective-permute-start(bf16[1,192,1536]{2,1,0:T(8,128)(2,1)} %get-tuple-element.45.refs_7_), channel_id=1, source_target_pairs={{0,1},{1,0},{2,3},{3,2},{4,5},{5,4},{6,7},{7,6}} | collective-permute-start | bytes 1769480 | tf_op jit(solution)/shard_map/ppermute | solution.py:670
  366.7 17.3 %collective-permute-start.11 = (bf16[1,192,768]{2,1,0:T(8,128)(2,1)}, bf16[1,192,768]{2,1,0:T(8,128)(2,1)S(1)}, u32[]{:S(2)}, u32[]{:S(2)}) collective-permute-start(bf16[1,192,768]{2,1,0:T(8,128)(2,1)} %get-tuple-element.52.refs_14_), channel_id=1, source_target_pairs={{0,1},{1,0},{2,3},{3,2},{4,5},{5,4},{6,7},{7,6}} | collective-permute-start | bytes 884744 | tf_op jit(solution)/shard_map/ppermute | solution.py:670
  369.5 15.2 %collective-permute-start.1 = (bf16[4,96,384]{2,1,0:T(8,128)(2,1)}, bf16[4,96,384]{2,1,0:T(8,128)(2,1)S(1)}, u32[]{:S(2)}, u32[]{:S(2)}) collective-permute-start(bf16[4,96,384]{2,1,0:T(8,128)(2,1)} %get-tuple-element.41.refs_2_), channel_id=1, source_target_pairs={{0,1},{1,0},{2,3},{3,2},{4,5},{5,4},{6,7},{7,6}} | collective-permute-start | bytes 884744 | tf_op jit(solution)/shard_map/ppermute | solution.py:669
  370.0 16.9 %copy-start.26 = (f32[4,192,1152]{2,1,0:T(8,128)S(1)}, f32[4,192,1152]{2,1,0:T(8,128)}, u32[]{:S(2)}) copy-start(f32[4,192,1152]{2,1,0:T(8,128)} %refs_5_.1) | copy-start | bytes 10616836
  370.0 16.9 %copy-start.27 = (f32[4,192,1152]{2,1,0:T(8,128)S(1)}, f32[4,192,1152]{2,1,0:T(8,128)}, u32[]{:S(2)}) copy-start(f32[4,192,1152]{2,1,0:T(8,128)} %refs_9_.1) | copy-start | bytes 10616836
  384.7 11.1 %collective-permute-start.7 = (bf16[1,384,768]{2,1,0:T(8,128)(2,1)S(1)}, bf16[1,384,768]{2,1,0:T(8,128)(2,1)S(1)}, u32[]{:S(2)}, u32[]{:S(2)}) collective-permute-start(bf16[1,384,768]{2,1,0:T(8,128)(2,1)S(1)} %copy-done.7), channel_id=1, source_target_pairs={{0,1},{1,0},{2,3},{3,2},{4,5},{5,4},{6,7},{7,6}} | collective-permute-start | bytes 1769480 | tf_op jit(solution)/shard_map/ppermute | solution.py:670
  384.7 16.3 %collective-permute-start.20 = (bf16[1,384,768]{2,1,0:T(8,128)(2,1)S(1)}, bf16[1,384,768]{2,1,0:T(8,128)(2,1)}, u32[]{:S(2)}, u32[]{:S(2)}) collective-permute-start(bf16[1,384,768]{2,1,0:T(8,128)(2,1)S(1)} %copy-done.7), channel_id=1, source_target_pairs={{0,2},{1,3},{2,0},{3,1},{4,6},{5,7},{6,4},{7,5}} | collective-permute-start | bytes 1769480 | tf_op jit(solution)/shard_map/ppermute | solution.py:666
  386.1 7.6 %collective-permute-start.5 = (bf16[1,192,1536]{2,1,0:T(8,128)(2,1)S(1)}, bf16[1,192,1536]{2,1,0:T(8,128)(2,1)}, u32[]{:S(2)}, u32[]{:S(2)}) collective-permute-start(bf16[1,192,1536]{2,1,0:T(8,128)(2,1)S(1)} %copy-done.4), channel_id=1, source_target_pairs={{0,1},{1,0},{2,3},{3,2},{4,5},{5,4},{6,7},{7,6}} | collective-permute-start | bytes 1769480 | tf_op jit(solution)/shard_map/ppermute | solution.py:670
  386.3 8.3 %collective-permute-start.6 = (bf16[1,192,1536]{2,1,0:T(8,128)(2,1)S(1)}, bf16[1,192,1536]{2,1,0:T(8,128)(2,1)}, u32[]{:S(2)}, u32[]{:S(2)}) collective-permute-start(bf16[1,192,1536]{2,1,0:T(8,128)(2,1)S(1)} %copy-done.2), channel_id=1, source_target_pairs={{0,1},{1,0},{2,3},{3,2},{4,5},{5,4},{6,7},{7,6}} | collective-permute-start | bytes 1769480 | tf_op jit(solution)/shard_map/ppermute | solution.py:670
  386.6 14.4 %collective-permute-start.8 = (bf16[1,384,768]{2,1,0:T(8,128)(2,1)}, bf16[1,384,768]{2,1,0:T(8,128)(2,1)}, u32[]{:S(2)}, u32[]{:S(2)}) collective-permute-start(bf16[1,384,768]{2,1,0:T(8,128)(2,1)} %get-tuple-element.49.refs_11_), channel_id=1, source_target_pairs={{0,1},{1,0},{2,3},{3,2},{4,5},{5,4},{6,7},{7,6}} | collective-permute-start | bytes 1769480 | tf_op jit(solution)/shard_map/ppermute | solution.py:670
  393.7 24.1 %collective-permute-start.22 = (bf16[1,384,768]{2,1,0:T(8,128)(2,1)}, bf16[1,384,768]{2,1,0:T(8,128)(2,1)}, u32[]{:S(2)}, u32[]{:S(2)}) collective-permute-start(bf16[1,384,768]{2,1,0:T(8,128)(2,1)} %get-tuple-element.49.refs_11_), channel_id=1, source_target_pairs={{0,2},{1,3},{2,0},{3,1},{4,6},{5,7},{6,4},{7,5}} | collective-permute-start | bytes 1769480 | tf_op jit(solution)/shard_map/ppermute | solution.py:666
  394.6 55.6 %collective-permute-start.12 = (bf16[1,192,1536]{2,1,0:T(8,128)(2,1)}, bf16[1,192,1536]{2,1,0:T(8,128)(2,1)}, u32[]{:S(2)}, u32[]{:S(2)}) collective-permute-start(bf16[1,192,1536]{2,1,0:T(8,128)(2,1)} %get-tuple-element.44.refs_6_), channel_id=1, source_target_pairs={{0,2},{1,3},{2,0},{3,1},{4,6},{5,7},{6,4},{7,5}} | collective-permute-start | bytes 1769480 | tf_op jit(solution)/shard_map/ppermute | solution.py:666
  396.5 19.0 %collective-permute-start.9 = (bf16[1,384,768]{2,1,0:T(8,128)(2,1)}, bf16[1,384,768]{2,1,0:T(8,128)(2,1)S(1)}, u32[]{:S(2)}, u32[]{:S(2)}) collective-permute-start(bf16[1,384,768]{2,1,0:T(8,128)(2,1)} %get-tuple-element.50.refs_12_), channel_id=1, source_target_pairs={{0,1},{1,0},{2,3},{3,2},{4,5},{5,4},{6,7},{7,6}} | collective-permute-start | bytes 1769480 | tf_op jit(solution)/shard_map/ppermute | solution.py:670
  401.0 50.5 %collective-permute-start.21 = (bf16[1,384,768]{2,1,0:T(8,128)(2,1)}, bf16[1,384,768]{2,1,0:T(8,128)(2,1)}, u32[]{:S(2)}, u32[]{:S(2)}) collective-permute-start(bf16[1,384,768]{2,1,0:T(8,128)(2,1)} %collective-permute-done.20), channel_id=1, source_target_pairs={{0,1},{1,0},{2,3},{3,2},{4,5},{5,4},{6,7},{7,6}} | collective-permute-start | bytes 1769480 | tf_op jit(solution)/shard_map/ppermute | solution.py:673
  401.0 19.8 %collective-permute-start.2 = (bf16[10,96,384]{2,1,0:T(8,128)(2,1)S(1)}, bf16[10,96,384]{2,1,0:T(8,128)(2,1)}, u32[]{:S(2)}, u32[]{:S(2)}) collective-permute-start(bf16[10,96,384]{2,1,0:T(8,128)(2,1)S(1)} %broadcast_select_fusion.refs_3_), channel_id=1, source_target_pairs={{0,1},{1,0},{2,3},{3,2},{4,5},{5,4},{6,7},{7,6}} | collective-permute-start | bytes 2211848 | tf_op jit(solution)/shard_map/ppermute | solution.py:669
  416.4 42.9 %collective-permute-start.24 = (bf16[1,384,768]{2,1,0:T(8,128)(2,1)}, bf16[1,384,768]{2,1,0:T(8,128)(2,1)}, u32[]{:S(2)}, u32[]{:S(2)}) collective-permute-start(bf16[1,384,768]{2,1,0:T(8,128)(2,1)} %get-tuple-element.50.refs_12_), channel_id=1, source_target_pairs={{0,2},{1,3},{2,0},{3,1},{4,6},{5,7},{6,4},{7,5}} | collective-permute-start | bytes 1769480 | tf_op jit(solution)/shard_map/ppermute | solution.py:666
  417.8 37.6 %collective-permute-start.23 = (bf16[1,384,768]{2,1,0:T(8,128)(2,1)}, bf16[1,384,768]{2,1,0:T(8,128)(2,1)}, u32[]{:S(2)}, u32[]{:S(2)}) collective-permute-start(bf16[1,384,768]{2,1,0:T(8,128)(2,1)} %collective-permute-done.22), channel_id=1, source_target_pairs={{0,1},{1,0},{2,3},{3,2},{4,5},{5,4},{6,7},{7,6}} | collective-permute-start | bytes 1769480 | tf_op jit(solution)/shard_map/ppermute | solution.py:673
  420.8 37.2 %collective-permute-start.26 = (bf16[1,192,768]{2,1,0:T(8,128)(2,1)}, bf16[1,192,768]{2,1,0:T(8,128)(2,1)S(1)}, u32[]{:S(2)}, u32[]{:S(2)}) collective-permute-start(bf16[1,192,768]{2,1,0:T(8,128)(2,1)} %get-tuple-element.51.refs_13_), channel_id=1, source_target_pairs={{0,2},{1,3},{2,0},{3,1},{4,6},{5,7},{6,4},{7,5}} | collective-permute-start | bytes 884744 | tf_op jit(solution)/shard_map/ppermute | solution.py:666
  450.2 47.0 %collective-permute-start.14 = (bf16[1,192,1536]{2,1,0:T(8,128)(2,1)S(1)}, bf16[1,192,1536]{2,1,0:T(8,128)(2,1)S(1)}, u32[]{:S(2)}, u32[]{:S(2)}) collective-permute-start(bf16[1,192,1536]{2,1,0:T(8,128)(2,1)S(1)} %copy-done.6), channel_id=1, source_target_pairs={{0,2},{1,3},{2,0},{3,1},{4,6},{5,7},{6,4},{7,5}} | collective-permute-start | bytes 1769480 | tf_op jit(solution)/shard_map/ppermute | solution.py:666
  451.5 9.7 %collective-permute-start.13 = (bf16[1,192,1536]{2,1,0:T(8,128)(2,1)}, bf16[1,192,1536]{2,1,0:T(8,128)(2,1)S(1)}, u32[]{:S(2)}, u32[]{:S(2)}) collective-permute-start(bf16[1,192,1536]{2,1,0:T(8,128)(2,1)} %collective-permute-done.12), channel_id=1, source_target_pairs={{0,1},{1,0},{2,3},{3,2},{4,5},{5,4},{6,7},{7,6}} | collective-permute-start | bytes 1769480 | tf_op jit(solution)/shard_map/ppermute | solution.py:673
  455.4 42.3 %collective-permute-start.16 = (bf16[1,192,1536]{2,1,0:T(8,128)(2,1)S(1)}, bf16[1,192,1536]{2,1,0:T(8,128)(2,1)S(1)}, u32[]{:S(2)}, u32[]{:S(2)}) collective-permute-start(bf16[1,192,1536]{2,1,0:T(8,128)(2,1)S(1)} %copy-done.5), channel_id=1, source_target_pairs={{0,2},{1,3},{2,0},{3,1},{4,6},{5,7},{6,4},{7,5}} | collective-permute-start | bytes 1769480 | tf_op jit(solution)/shard_map/ppermute | solution.py:666
  457.9 39.8 %collective-permute-start.18 = (bf16[1,192,1536]{2,1,0:T(8,128)(2,1)S(1)}, bf16[1,192,1536]{2,1,0:T(8,128)(2,1)S(1)}, u32[]{:S(2)}, u32[]{:S(2)}) collective-permute-start(bf16[1,192,1536]{2,1,0:T(8,128)(2,1)S(1)} %copy-done.3), channel_id=1, source_target_pairs={{0,2},{1,3},{2,0},{3,1},{4,6},{5,7},{6,4},{7,5}} | collective-permute-start | bytes 1769480 | tf_op jit(solution)/shard_map/ppermute | solution.py:666
  459.3 38.9 %collective-permute-start.25 = (bf16[1,384,768]{2,1,0:T(8,128)(2,1)}, bf16[1,384,768]{2,1,0:T(8,128)(2,1)S(1)}, u32[]{:S(2)}, u32[]{:S(2)}) collective-permute-start(bf16[1,384,768]{2,1,0:T(8,128)(2,1)} %collective-permute-done.24), channel_id=1, source_target_pairs={{0,1},{1,0},{2,3},{3,2},{4,5},{5,4},{6,7},{7,6}} | collective-permute-start | bytes 1769480 | tf_op jit(solution)/shard_map/ppermute | solution.py:673
  461.2 36.0 %collective-permute-start.28 = (bf16[1,192,768]{2,1,0:T(8,128)(2,1)S(1)}, bf16[1,192,768]{2,1,0:T(8,128)(2,1)S(1)}, u32[]{:S(2)}, u32[]{:S(2)}) collective-permute-start(bf16[1,192,768]{2,1,0:T(8,128)(2,1)S(1)} %copy-done.17), channel_id=1, source_target_pairs={{0,2},{1,3},{2,0},{3,1},{4,6},{5,7},{6,4},{7,5}} | collective-permute-start | bytes 884744 | tf_op jit(solution)/shard_map/ppermute | solution.py:666
  497.2 3.5 collective-permute-start.27
  497.2 9.2 %collective-permute-start.29 = (bf16[1,192,768]{2,1,0:T(8,128)(2,1)S(1)}, bf16[1,192,768]{2,1,0:T(8,128)(2,1)S(1)}, u32[]{:S(2)}, u32[]{:S(2)}) collective-permute-start(bf16[1,192,768]{2,1,0:T(8,128)(2,1)S(1)} %collective-permute-done.28), channel_id=1, source_target_pairs={{0,1},{1,0},{2,3},{3,2},{4,5},{5,4},{6,7},{7,6}} | collective-permute-start | bytes 884744 | tf_op jit(solution)/shard_map/ppermute | solution.py:673
  497.7 3.7 collective-permute-start.15
  497.7 5.4 %collective-permute-start.17 = (bf16[1,192,1536]{2,1,0:T(8,128)(2,1)S(1)}, bf16[1,192,1536]{2,1,0:T(8,128)(2,1)S(1)}, u32[]{:S(2)}, u32[]{:S(2)}) collective-permute-start(bf16[1,192,1536]{2,1,0:T(8,128)(2,1)S(1)} %collective-permute-done.16), channel_id=1, source_target_pairs={{0,1},{1,0},{2,3},{3,2},{4,5},{5,4},{6,7},{7,6}} | collective-permute-start | bytes 1769480 | tf_op jit(solution)/shard_map/ppermute | solution.py:673
  498.2 7.4 %collective-permute-start.19 = (bf16[1,192,1536]{2,1,0:T(8,128)(2,1)S(1)}, bf16[1,192,1536]{2,1,0:T(8,128)(2,1)S(1)}, u32[]{:S(2)}, u32[]{:S(2)}) collective-permute-start(bf16[1,192,1536]{2,1,0:T(8,128)(2,1)S(1)} %collective-permute-done.18), channel_id=1, source_target_pairs={{0,1},{1,0},{2,3},{3,2},{4,5},{5,4},{6,7},{7,6}} | collective-permute-start | bytes 1769480 | tf_op jit(solution)/shard_map/ppermute | solution.py:673
  (33 other events, 203.0 us)

commit v3 on v2

--- a/solution.py
+++ b/solution.py
@@ -46,6 +46,7 @@
 TAIL_GROUPS = 5
 TAIL_FIRST = SENT_GROUPS - TAIL_GROUPS
 RELAYED = TAIL_FIRST - LATE_GROUPS
+AHEAD = 1
 LAST_ROWS = 192
 PIECES = tuple(
     [(layer, 0, SHARD_ROWS[kind]) for layer in range(LAYERS - (kind == FCOUT))]
@@ -116,9 +117,9 @@
 
 def step_kernel(*refs):
     counts = tuple(map(len, PIECES))
-    grads, weights, firsts, seconds, means, reps, in_pieces, out_pieces, rest = split(refs, *[len(KINDS)] * 5, PAIR, *counts, 22)
+    grads, weights, firsts, seconds, means, reps, in_pieces, out_pieces, rest = split(refs, *[len(KINDS)] * 5, PAIR, *counts, 23)
     pieces = {FCIN: in_pieces, FCOUT: out_pieces}
-    (late, tail, extra, scal_out, recv, stage, mean, held, ring, note, notes, w_sums, u_sums, n_sum, scal,
+    (late, tail, extra, scal_out, recv, ahead, stage, mean, held, ring, note, notes, w_sums, u_sums, n_sum, scal,
      ring_sem, held_sem, mean_sem, send_sem, recv_sem, rep_send_sem, note_sem) = rest
     model, data = lax.axis_index("model"), lax.axis_index("data")
     partner = partners(data)
@@ -187,7 +188,7 @@
         count = len(OTHERS) * PAIR
         return remote(landed(count), landed(count), send_sem.at[group % SEND_SLOTS], recv_sem.at[group], FAR)
 
-    early = PAIR * PAIR
+    early = PAIR
     for unit in range(early):
         start_grads_static(unit, grads, ring, ring_sem, partner)
 
@@ -199,7 +200,6 @@
 
     for peer in peers:
         pl.semaphore_signal(barrier, inc=1, device_id=device(peer), device_id_type=MESH)
-    pl.semaphore_wait(barrier, len(peers))
     for unit in range(early, RING):
         start_grads_static(unit, grads, ring, ring_sem, partner)
 
@@ -262,6 +262,10 @@
             for_kind(unit, KINDS, body)
             start_mean_out(unit)
 
+    convert(0)
+    keep_own(0)
+    pl.semaphore_wait(barrier, len(peers))
+
     def exchange_step(group, _):
         for j in range(PAIR):
             start_weight(PAIR * group + j)
@@ -270,8 +274,11 @@
         def _():
             grad_copies(group - SEND_SLOTS).wait_send()
 
-        convert(group)
-        keep_own(group)
+        @pl.when(group >= 1)
+        def _():
+            convert(group)
+            keep_own(group)
+
         for k in (FAR, CROSS, NEAR):
             grad_copy(group, k).start()
 
@@ -317,6 +324,10 @@
         remote(arrived, arrived, note_sem.at[0, index], note_sem.at[1, index], FAR).wait()
         return note[index] + jnp.sum(notes[index], axis=0)
 
+    def ahead_copy(part, first_row=0, end_row=UNIT_ROWS):
+        rows, sem = pl.ds(first_row, end_row - first_row), len(KINDS) + PAIR + part
+        return remote((held, mean)[part].at[AHEAD, rows], ahead.at[part, rows], note_sem.at[0, sem], note_sem.at[1, sem], FAR)
+
     note[n_note] = n_sum[...]
 
     def settle(group, _):
@@ -325,6 +336,7 @@
 
     lax.fori_loop(GROUPS - SEND_SLOTS, GROUPS, settle, 0)
     send_note(n_note)
+    ahead_copy(0).start()
 
     def settle_means(group, _):
         wait_mean_out(group)
@@ -395,12 +407,21 @@
 
         lax.fori_loop(unit_from, unit_to, unit_step, 0)
 
+    def weights_ahead():
+        ratio = LEARN_RATE * scal[PROJ, AHEAD // BLOCKS[PROJ]:AHEAD // BLOCKS[PROJ] + 1, :][:, :1]
+        for i in range(0, UNIT_ROWS, CHUNK):
+            at = pl.ds(i, CHUNK)
+            recv[FAR - 1, AHEAD, at, :] = (ahead[0, at, :] - ratio * ahead[1, at, :]).astype(BF16)
+
     near_sem = PAIR * SENT_GROUPS
 
     def rep_copy(group, k):
         source = recv.at[FAR - 1, pair(group)] if k == CROSS else stage.at[pair(group)]
         arrival = {NEAR: near_sem, FAR: group, CROSS: SENT_GROUPS + group}[k]
         return remote(source, recv.at[k - 1, pair(group)], rep_send_sem.at[k - 1], recv_sem.at[arrival], FAR if k == FAR else NEAR)
+
+    def first_copy():
+        return remote(stage.at[0], recv.at[FAR - 1, 0], rep_send_sem.at[FAR - 1], recv_sem.at[0], FAR)
 
     def late_copy(group):
         target = late.at[pair(group - RELAYED)] if group < TAIL_FIRST else tail.at[pair(group - TAIL_FIRST)]
@@ -450,22 +471,27 @@
     write_early_note()
     refill(0, first)
     send_note(early_note)
+    ahead_copy(1, 0, CHUNK * PAIR).start()
     directions(PROJ, first, proj_end)
     write_note(PROJ)
-    directions(QKV, 0, PAIR)
+    refill(first, PAIR * first)
     send_note(PROJ)
-    directions(QKV, PAIR, half)
+    ahead_copy(1, CHUNK * PAIR).start()
+    directions(QKV, 0, half)
     early_ratio()
     new_weights(PROJ, 0, first, stage)
-    refill(first, PAIR * first)
-    start_replicas(0, first)
+    refill(PAIR * first, PAIR * first + PAIR)
+    first_copy().start()
+    rep_copy(0, NEAR).start()
     ratios(PROJ)
     new_weights(PROJ, first, proj_end, stage)
+    refill(PAIR * first + PAIR, proj_end)
+    start_replicas(first, PAIR * first)
     directions(QKV, half, qkv_end)
-    start_replicas(first, PAIR * first)
     write_note(QKV)
-    refill(PAIR * first, SENT_UNITS)
+    refill(proj_end, proj_end + PAIR)
     send_note(QKV)
+    refill(proj_end + PAIR, SENT_UNITS)
     start_replicas(PAIR * first, proj_end)
     directions(FCIN, 0, piece_end // PAIR)
     ratios(QKV)
@@ -484,6 +510,9 @@
     send_note(FCOUT)
     start_replicas(proj_end + half // PAIR, PAIR * RELAYED)
     start_late_replicas()
+    for part in range(PAIR):
+        ahead_copy(part).wait()
+    weights_ahead()
     replicas_out(0, SENT_UNITS, OWN)
     for kind in (FCIN, FCOUT):
         ratios(kind)
@@ -498,7 +527,14 @@
     def relay_step(group, _):
         @pl.when(group < RELAYED)
         def _():
-            rep_copy(group, FAR).wait_recv()
+            @pl.when(group == 0)
+            def _():
+                first_copy().wait_recv()
+
+            @pl.when(group >= 1)
+            def _():
+                rep_copy(group, FAR).wait_recv()
+
             rep_copy(group, CROSS).start()
             replicas_out(PAIR * group, PAIR * group + PAIR, FAR)
 
@@ -520,13 +556,13 @@
 
     @pl.when(stays)
     def _():
-        all_copies(FAR, SENT_UNITS).wait_send()
+        all_copies(FAR, SENT_UNITS - 1).wait_send()
         for group in range(TAIL_FIRST, SENT_GROUPS):
             late_copy(group).wait_recv()
 
     @pl.when(jnp.logical_not(stays))
     def _():
-        all_copies(FAR, PAIR * TAIL_FIRST).wait_send()
+        all_copies(FAR, PAIR * TAIL_FIRST - 1).wait_send()
 
 
 def place_static(kind, index):
@@ -537,7 +573,7 @@
 def start_grads_static(unit, grads, ring, ring_sem, partner):
     kind = next(kind for kind in KINDS if unit < FIRST[kind + 1])
     layer, row, col = place_static(kind, unit - FIRST[kind])
-    for k in PARTNERS:
+    for k in (FAR, CROSS, NEAR, OWN):
         base = pl.multiple_of(partner[k] * SHARD_ROWS[kind] + row, UNIT_ROWS)
         pltpu.make_async_copy(grads[kind].at[0, layer, pl.ds(base, UNIT_ROWS), pl.ds(col, UNIT_COLS)], ring.at[unit, k], ring_sem.at[unit]).start()
 
@@ -637,6 +673,7 @@
             out_specs=[any_spec] * len(out_shape),
             scratch_shapes=[
                 pltpu.VMEM((len(OTHERS), UNITS) + unit, BF16),
+                pltpu.VMEM((PAIR,) + unit, F32),
                 pltpu.VMEM((len(OTHERS) * PAIR * SEND_SLOTS,) + unit, BF16),
                 pltpu.VMEM((UNITS,) + unit, F32),
                 pltpu.VMEM((UNITS,) + unit, F32),
@@ -647,7 +684,7 @@
                 pltpu.VMEM((LAYERS * len(KINDS),) + TILE, F32),
                 pltpu.VMEM(TILE, F32),
                 pltpu.VMEM(scal_shape, F32),
-                dma((RING,)), dma((RING,)), dma((SEND_SLOTS,)), dma((SEND_SLOTS,)), dma((GROUPS,)), dma((len(OTHERS),)), dma((PAIR, messages)),
+                dma((RING,)), dma((RING,)), dma((SEND_SLOTS,)), dma((SEND_SLOTS,)), dma((GROUPS,)), dma((len(OTHERS),)), dma((PAIR, messages + PAIR)),
             ],
             compiler_params=pltpu.CompilerParams(collective_id=0, has_side_effects=True, vmem_limit_bytes=66_900_000),
         )(*operands)

time: 508 us -> 507 us (level)
  no operation moved by 1% of the time
where the time goes in v3:
time: 507 us; the launch traced here: 506 us
  Pallas kernels  364 us (72%)
  local copies, waits for them, and re-layouts  41.9 us (8%)
  other arithmetic  38.6 us (8%)
  waiting for transfers between devices  37 us (7%)
  starting transfers between devices  23 us (5%)
    pallas_call x1, Pallas kernels, device_step(): pl.pallas_call(step_kernel, out_shape=out_shape, in_specs=[any_spec] * le...  354 us
    ppermute x9, waiting for transfers between devices, device_step(): far.append(lax.ppermute(piece, 'data', across))  36.9 us
    sub x4, other arithmetic, device_step(): state[kind] = (weight - LEARN_RATE * ratio * update, new_first, new_second)  36.5 us
    dynamic_update_slice x18, local copies, waits for them, and re-layouts, device_step(): lax.dynamic_update_slice(replicas[kind], piece, (layer, owners[k] * SHARD...  21.3 us
    unnamed x70, local copies, waits for them, and re-layouts  19.4 us
    pallas_call x1, Pallas kernels, assemble(): pl.pallas_call(assemble_kernel, out_shape=[shape(s, BF16) for s in whole]...  10.4 us
  transfers between devices with their start and end apart: 30, of which 2 were waited for; matrix products, arithmetic and copies ran while one was open for 12% of the time, Pallas kernels for 2%

profile of v3, /device:TPU:0, one launch (start us, length us, event | category | flops | bytes accessed | tf_op | source)
XLA Modules:
  0.0 505.5 jit_solution(5675663665330540220)
XLA Ops:
  0.6 353.7 %shard_map.279 = (f32[4,96,768]{2,1,0:T(8,128)}, f32[4,192,1152]{2,1,0:T(8,128)}, f32[4,192,1536]{2,1,0:T(8,128)}, f32[4,384,768]{2,1,0:T(8,128)}, bf16[4,384,76...) custom-call(f32[1,4,384,768]{3,2,1,0:T(8,128)} %refs_0_.1, ...), custom_call_target="tpu_custom_call" | custom-call | tf_op jit(solution)/shard_map/pallas_call | solution.py:669
  354.4 7.4 %collective-permute-start.10 = (bf16[1,192,768]{2,1,0:T(8,128)(2,1)}, bf16[1,192,768]{2,1,0:T(8,128)(2,1)S(1)}, u32[]{:S(2)}, u32[]{:S(2)}) collective-permute-start(bf16[1,192,768]{2,1,0:T(8,128)(2,1)} %get-tuple-element.51.refs_13_), channel_id=1, source_target_pairs={{0,1},{1,0},{2,3},{3,2},{4,5},{5,4},{6,7},{7,6}} | collective-permute-start | bytes 884744 | tf_op jit(solution)/shard_map/ppermute | solution.py:707
  361.8 2.7 collective-permute-start
  365.0 1.2 slice.16
  368.3 14.0 %multiply_subtract_fusion.1 = (f32[4,192,1536]{2,1,0:T(8,128)}, f32[4,192,1536]{2,1,0:T(8,128)}, f32[4,192,1536]{2,1,0:T(8,128)}) fusion(f32[4,192,1536]{2,1,0:T(8,128)} %refs_6_.1, f32[4]{0:T(128)S(1)} %get-tuple-element.63, f32[4,192,1536]{2,1,0:T(8,128)} %get-tuple-element.60, f32[]{:T(128)} %bitcast, f32[4,192,1536]{2,1,0:T(8,128)} %refs_10_.1, ...), kind=kLoop, calls=%fused_computation.7 | loop fusion | flops 18874368 | bytes 33030164 | tf_op jit(solution)/shard_map/sub | solution.py:700
  383.0 1.4 collective-permute-start.20
  385.3 5.6 %multiply_subtract_fusion.2 = (f32[4,192,1152]{2,1,0:T(8,128)}, f32[4,192,1152]{2,1,0:T(8,128)}, f32[4,192,1152]{2,1,0:T(8,128)}) fusion(f32[4,192,1152]{2,1,0:T(8,128)S(1)} %copy-done.26, f32[4]{0:T(128)S(1)} %get-tuple-element.65, f32[4,192,1152]{2,1,0:T(8,128)S(1)} %copy-done.32, f32[]{:T(128)} %bitcast, f32[4,192,1152]{2,1,0:T(8,128)S(1)} %copy-done.27, ...), kind=kLoop, calls=%fused_computation.10 | loop fusion | flops 14155776 | bytes 24772628 | tf_op jit(solution)/shard_map/sub | solution.py:700
  390.9 1.2 broadcast_select_fusion.refs_3_
  393.0 1.1 collective-permute-start.12
  395.0 4.4 collective-permute-done.20
  399.9 14.0 %multiply_subtract_fusion = (f32[4,384,768]{2,1,0:T(8,128)}, f32[4,384,768]{2,1,0:T(8,128)}, f32[4,384,768]{2,1,0:T(8,128)}) fusion(f32[4,384,768]{2,1,0:T(8,128)} %refs_7_.1, f32[4]{0:T(128)S(1)} %get-tuple-element.62, f32[4,384,768]{2,1,0:T(8,128)} %get-tuple-element.61, f32[]{:T(128)} %bitcast, f32[4,384,768]{2,1,0:T(8,128)} %refs_11_.1, ...), kind=kLoop, calls=%fused_computation.5 | loop fusion | flops 18874368 | bytes 33030164 | tf_op jit(solution)/shard_map/sub | solution.py:700
  414.7 1.4 collective-permute-start.24
  416.2 3.0 multiply_subtract_fusion.3
  419.8 3.0 copy-done
  422.8 1.1 copy-done.3
  423.9 1.1 copy-done.5
  424.9 1.1 copy-done.6
  426.0 1.1 copy-done.8
  427.1 1.1 copy-done.10
  428.1 1.1 copy-done.12
  429.2 1.1 copy-done.14
  430.3 1.1 copy-done.16
  436.1 10.4 %shard_map.280 = (bf16[4,384,768]{2,1,0:T(8,128)(2,1)}, bf16[4,768,1152]{2,1,0:T(8,128)(2,1)}, bf16[4,768,1536]{2,1,0:T(8,128)(2,1)}, bf16[4,1536,768]{2,1,0:T(8,128)(2,1)}) custom-call(bf16[4,384,768]{2,1,0:T(8,128)(2,1)S(1)} %copy-done.1, bf16[4,768,1152]{2,1,0:T(8,128)(2,1)S(1)} %copy-done, bf16[4,96,384]{2,1,0:T(8,128)(2,1)S(1)} %copy-done.19, ...), custom_call_target="tpu_custom_call" | custom-call | flops 12000000 | bytes 38000000 | tf_op jit(solution)/shard_map/pallas_call | solution.py:629
  446.6 1.9 constant_dynamic-update-slice_fusion.9
  448.5 1.4 collective-permute-start.14
  450.0 1.9 constant_dynamic-update-slice_fusion.8
  451.9 1.9 constant_dynamic-update-slice_fusion.7
  454.4 1.9 constant_dynamic-update-slice_fusion.6
  456.3 1.4 collective-permute-start.18
  457.7 1.9 constant_dynamic-update-slice_fusion.17
  460.2 1.9 constant_dynamic-update-slice_fusion.5
  463.0 32.5 %collective-permute-done.28 = bf16[1,192,768]{2,1,0:T(8,128)(2,1)S(1)} collective-permute-done((bf16[1,192,768]{2,1,0:T(8,128)(2,1)S(1)}, bf16[1,192,768]{2,1,0:T(8,128)(2,1)S(1)}, u32[]{:S(2)}, u32[]{:S(2)}) %collective-permute-start.28) | collective-permute-done | bytes 294944 | tf_op jit(solution)/shard_map/ppermute | solution.py:703
  (125 shorter events, 24.6 us)
Async XLA Ops:
  354.4 12.7 %collective-permute-start.10 = (bf16[1,192,768]{2,1,0:T(8,128)(2,1)}, bf16[1,192,768]{2,1,0:T(8,128)(2,1)S(1)}, u32[]{:S(2)}, u32[]{:S(2)}) collective-permute-start(bf16[1,192,768]{2,1,0:T(8,128)(2,1)} %get-tuple-element.51.refs_13_), channel_id=1, source_target_pairs={{0,1},{1,0},{2,3},{3,2},{4,5},{5,4},{6,7},{7,6}} | collective-permute-start | bytes 884744 | tf_op jit(solution)/shard_map/ppermute | solution.py:707
  361.8 23.3 %collective-permute-start = (bf16[10,96,384]{2,1,0:T(8,128)(2,1)}, bf16[10,96,384]{2,1,0:T(8,128)(2,1)S(1)}, u32[]{:S(2)}, u32[]{:S(2)}) collective-permute-start(bf16[10,96,384]{2,1,0:T(8,128)(2,1)} %get-tuple-element.42), channel_id=1, source_target_pairs={{0,2},{2,0},{4,6},{6,4}} | collective-permute-start | bytes 2211848 | tf_op jit(solution)/shard_map/ppermute | solution.py:704
  364.5 20.0 %collective-permute-start.3 = (bf16[1,192,1536]{2,1,0:T(8,128)(2,1)}, bf16[1,192,1536]{2,1,0:T(8,128)(2,1)S(1)}, u32[]{:S(2)}, u32[]{:S(2)}) collective-permute-start(bf16[1,192,1536]{2,1,0:T(8,128)(2,1)} %get-tuple-element.44.refs_6_), channel_id=1, source_target_pairs={{0,1},{1,0},{2,3},{3,2},{4,5},{5,4},{6,7},{7,6}} | collective-permute-start | bytes 1769480 | tf_op jit(solution)/shard_map/ppermute | solution.py:707
  364.5 20.2 %collective-permute-start.4 = (bf16[1,192,1536]{2,1,0:T(8,128)(2,1)}, bf16[1,192,1536]{2,1,0:T(8,128)(2,1)S(1)}, u32[]{:S(2)}, u32[]{:S(2)}) collective-permute-start(bf16[1,192,1536]{2,1,0:T(8,128)(2,1)} %get-tuple-element.45.refs_7_), channel_id=1, source_target_pairs={{0,1},{1,0},{2,3},{3,2},{4,5},{5,4},{6,7},{7,6}} | collective-permute-start | bytes 1769480 | tf_op jit(solution)/shard_map/ppermute | solution.py:707
  365.0 17.3 %collective-permute-start.11 = (bf16[1,192,768]{2,1,0:T(8,128)(2,1)}, bf16[1,192,768]{2,1,0:T(8,128)(2,1)S(1)}, u32[]{:S(2)}, u32[]{:S(2)}) collective-permute-start(bf16[1,192,768]{2,1,0:T(8,128)(2,1)} %get-tuple-element.52.refs_14_), channel_id=1, source_target_pairs={{0,1},{1,0},{2,3},{3,2},{4,5},{5,4},{6,7},{7,6}} | collective-permute-start | bytes 884744 | tf_op jit(solution)/shard_map/ppermute | solution.py:707
  367.8 15.2 %collective-permute-start.1 = (bf16[4,96,384]{2,1,0:T(8,128)(2,1)}, bf16[4,96,384]{2,1,0:T(8,128)(2,1)S(1)}, u32[]{:S(2)}, u32[]{:S(2)}) collective-permute-start(bf16[4,96,384]{2,1,0:T(8,128)(2,1)} %get-tuple-element.41.refs_2_), channel_id=1, source_target_pairs={{0,1},{1,0},{2,3},{3,2},{4,5},{5,4},{6,7},{7,6}} | collective-permute-start | bytes 884744 | tf_op jit(solution)/shard_map/ppermute | solution.py:706
  368.3 17.0 %copy-start.26 = (f32[4,192,1152]{2,1,0:T(8,128)S(1)}, f32[4,192,1152]{2,1,0:T(8,128)}, u32[]{:S(2)}) copy-start(f32[4,192,1152]{2,1,0:T(8,128)} %refs_5_.1) | copy-start | bytes 10616836
  368.3 17.0 %copy-start.27 = (f32[4,192,1152]{2,1,0:T(8,128)S(1)}, f32[4,192,1152]{2,1,0:T(8,128)}, u32[]{:S(2)}) copy-start(f32[4,192,1152]{2,1,0:T(8,128)} %refs_9_.1) | copy-start | bytes 10616836
  383.0 11.1 %collective-permute-start.7 = (bf16[1,384,768]{2,1,0:T(8,128)(2,1)S(1)}, bf16[1,384,768]{2,1,0:T(8,128)(2,1)S(1)}, u32[]{:S(2)}, u32[]{:S(2)}) collective-permute-start(bf16[1,384,768]{2,1,0:T(8,128)(2,1)S(1)} %copy-done.7), channel_id=1, source_target_pairs={{0,1},{1,0},{2,3},{3,2},{4,5},{5,4},{6,7},{7,6}} | collective-permute-start | bytes 1769480 | tf_op jit(solution)/shard_map/ppermute | solution.py:707
  383.0 16.3 %collective-permute-start.20 = (bf16[1,384,768]{2,1,0:T(8,128)(2,1)S(1)}, bf16[1,384,768]{2,1,0:T(8,128)(2,1)}, u32[]{:S(2)}, u32[]{:S(2)}) collective-permute-start(bf16[1,384,768]{2,1,0:T(8,128)(2,1)S(1)} %copy-done.7), channel_id=1, source_target_pairs={{0,2},{1,3},{2,0},{3,1},{4,6},{5,7},{6,4},{7,5}} | collective-permute-start | bytes 1769480 | tf_op jit(solution)/shard_map/ppermute | solution.py:703
  384.5 7.6 %collective-permute-start.5 = (bf16[1,192,1536]{2,1,0:T(8,128)(2,1)S(1)}, bf16[1,192,1536]{2,1,0:T(8,128)(2,1)}, u32[]{:S(2)}, u32[]{:S(2)}) collective-permute-start(bf16[1,192,1536]{2,1,0:T(8,128)(2,1)S(1)} %copy-done.4), channel_id=1, source_target_pairs={{0,1},{1,0},{2,3},{3,2},{4,5},{5,4},{6,7},{7,6}} | collective-permute-start | bytes 1769480 | tf_op jit(solution)/shard_map/ppermute | solution.py:707
  384.7 8.3 %collective-permute-start.6 = (bf16[1,192,1536]{2,1,0:T(8,128)(2,1)S(1)}, bf16[1,192,1536]{2,1,0:T(8,128)(2,1)}, u32[]{:S(2)}, u32[]{:S(2)}) collective-permute-start(bf16[1,192,1536]{2,1,0:T(8,128)(2,1)S(1)} %copy-done.2), channel_id=1, source_target_pairs={{0,1},{1,0},{2,3},{3,2},{4,5},{5,4},{6,7},{7,6}} | collective-permute-start | bytes 1769480 | tf_op jit(solution)/shard_map/ppermute | solution.py:707
  385.1 14.3 %collective-permute-start.8 = (bf16[1,384,768]{2,1,0:T(8,128)(2,1)}, bf16[1,384,768]{2,1,0:T(8,128)(2,1)}, u32[]{:S(2)}, u32[]{:S(2)}) collective-permute-start(bf16[1,384,768]{2,1,0:T(8,128)(2,1)} %get-tuple-element.49.refs_11_), channel_id=1, source_target_pairs={{0,1},{1,0},{2,3},{3,2},{4,5},{5,4},{6,7},{7,6}} | collective-permute-start | bytes 1769480 | tf_op jit(solution)/shard_map/ppermute | solution.py:707
  392.1 24.1 %collective-permute-start.22 = (bf16[1,384,768]{2,1,0:T(8,128)(2,1)}, bf16[1,384,768]{2,1,0:T(8,128)(2,1)}, u32[]{:S(2)}, u32[]{:S(2)}) collective-permute-start(bf16[1,384,768]{2,1,0:T(8,128)(2,1)} %get-tuple-element.49.refs_11_), channel_id=1, source_target_pairs={{0,2},{1,3},{2,0},{3,1},{4,6},{5,7},{6,4},{7,5}} | collective-permute-start | bytes 1769480 | tf_op jit(solution)/shard_map/ppermute | solution.py:703
  393.0 55.5 %collective-permute-start.12 = (bf16[1,192,1536]{2,1,0:T(8,128)(2,1)}, bf16[1,192,1536]{2,1,0:T(8,128)(2,1)}, u32[]{:S(2)}, u32[]{:S(2)}) collective-permute-start(bf16[1,192,1536]{2,1,0:T(8,128)(2,1)} %get-tuple-element.44.refs_6_), channel_id=1, source_target_pairs={{0,2},{1,3},{2,0},{3,1},{4,6},{5,7},{6,4},{7,5}} | collective-permute-start | bytes 1769480 | tf_op jit(solution)/shard_map/ppermute | solution.py:703
  395.0 18.9 %collective-permute-start.9 = (bf16[1,384,768]{2,1,0:T(8,128)(2,1)}, bf16[1,384,768]{2,1,0:T(8,128)(2,1)S(1)}, u32[]{:S(2)}, u32[]{:S(2)}) collective-permute-start(bf16[1,384,768]{2,1,0:T(8,128)(2,1)} %get-tuple-element.50.refs_12_), channel_id=1, source_target_pairs={{0,1},{1,0},{2,3},{3,2},{4,5},{5,4},{6,7},{7,6}} | collective-permute-start | bytes 1769480 | tf_op jit(solution)/shard_map/ppermute | solution.py:707
  399.4 50.6 %collective-permute-start.21 = (bf16[1,384,768]{2,1,0:T(8,128)(2,1)}, bf16[1,384,768]{2,1,0:T(8,128)(2,1)}, u32[]{:S(2)}, u32[]{:S(2)}) collective-permute-start(bf16[1,384,768]{2,1,0:T(8,128)(2,1)} %collective-permute-done.20), channel_id=1, source_target_pairs={{0,1},{1,0},{2,3},{3,2},{4,5},{5,4},{6,7},{7,6}} | collective-permute-start | bytes 1769480 | tf_op jit(solution)/shard_map/ppermute | solution.py:710
  399.4 19.9 %collective-permute-start.2 = (bf16[10,96,384]{2,1,0:T(8,128)(2,1)S(1)}, bf16[10,96,384]{2,1,0:T(8,128)(2,1)}, u32[]{:S(2)}, u32[]{:S(2)}) collective-permute-start(bf16[10,96,384]{2,1,0:T(8,128)(2,1)S(1)} %broadcast_select_fusion.refs_3_), channel_id=1, source_target_pairs={{0,1},{1,0},{2,3},{3,2},{4,5},{5,4},{6,7},{7,6}} | collective-permute-start | bytes 2211848 | tf_op jit(solution)/shard_map/ppermute | solution.py:706
  414.7 43.0 %collective-permute-start.24 = (bf16[1,384,768]{2,1,0:T(8,128)(2,1)}, bf16[1,384,768]{2,1,0:T(8,128)(2,1)}, u32[]{:S(2)}, u32[]{:S(2)}) collective-permute-start(bf16[1,384,768]{2,1,0:T(8,128)(2,1)} %get-tuple-element.50.refs_12_), channel_id=1, source_target_pairs={{0,2},{1,3},{2,0},{3,1},{4,6},{5,7},{6,4},{7,5}} | collective-permute-start | bytes 1769480 | tf_op jit(solution)/shard_map/ppermute | solution.py:703
  416.2 37.6 %collective-permute-start.23 = (bf16[1,384,768]{2,1,0:T(8,128)(2,1)}, bf16[1,384,768]{2,1,0:T(8,128)(2,1)}, u32[]{:S(2)}, u32[]{:S(2)}) collective-permute-start(bf16[1,384,768]{2,1,0:T(8,128)(2,1)} %collective-permute-done.22), channel_id=1, source_target_pairs={{0,1},{1,0},{2,3},{3,2},{4,5},{5,4},{6,7},{7,6}} | collective-permute-start | bytes 1769480 | tf_op jit(solution)/shard_map/ppermute | solution.py:710
  419.2 37.1 %collective-permute-start.26 = (bf16[1,192,768]{2,1,0:T(8,128)(2,1)}, bf16[1,192,768]{2,1,0:T(8,128)(2,1)S(1)}, u32[]{:S(2)}, u32[]{:S(2)}) collective-permute-start(bf16[1,192,768]{2,1,0:T(8,128)(2,1)} %get-tuple-element.51.refs_13_), channel_id=1, source_target_pairs={{0,2},{1,3},{2,0},{3,1},{4,6},{5,7},{6,4},{7,5}} | collective-permute-start | bytes 884744 | tf_op jit(solution)/shard_map/ppermute | solution.py:703
  448.5 47.0 %collective-permute-start.14 = (bf16[1,192,1536]{2,1,0:T(8,128)(2,1)S(1)}, bf16[1,192,1536]{2,1,0:T(8,128)(2,1)S(1)}, u32[]{:S(2)}, u32[]{:S(2)}) collective-permute-start(bf16[1,192,1536]{2,1,0:T(8,128)(2,1)S(1)} %copy-done.6), channel_id=1, source_target_pairs={{0,2},{1,3},{2,0},{3,1},{4,6},{5,7},{6,4},{7,5}} | collective-permute-start | bytes 1769480 | tf_op jit(solution)/shard_map/ppermute | solution.py:703
  450.0 9.7 %collective-permute-start.13 = (bf16[1,192,1536]{2,1,0:T(8,128)(2,1)}, bf16[1,192,1536]{2,1,0:T(8,128)(2,1)S(1)}, u32[]{:S(2)}, u32[]{:S(2)}) collective-permute-start(bf16[1,192,1536]{2,1,0:T(8,128)(2,1)} %collective-permute-done.12), channel_id=1, source_target_pairs={{0,1},{1,0},{2,3},{3,2},{4,5},{5,4},{6,7},{7,6}} | collective-permute-start | bytes 1769480 | tf_op jit(solution)/shard_map/ppermute | solution.py:710
  453.8 42.3 %collective-permute-start.16 = (bf16[1,192,1536]{2,1,0:T(8,128)(2,1)S(1)}, bf16[1,192,1536]{2,1,0:T(8,128)(2,1)S(1)}, u32[]{:S(2)}, u32[]{:S(2)}) collective-permute-start(bf16[1,192,1536]{2,1,0:T(8,128)(2,1)S(1)} %copy-done.5), channel_id=1, source_target_pairs={{0,2},{1,3},{2,0},{3,1},{4,6},{5,7},{6,4},{7,5}} | collective-permute-start | bytes 1769480 | tf_op jit(solution)/shard_map/ppermute | solution.py:703
  456.3 39.8 %collective-permute-start.18 = (bf16[1,192,1536]{2,1,0:T(8,128)(2,1)S(1)}, bf16[1,192,1536]{2,1,0:T(8,128)(2,1)S(1)}, u32[]{:S(2)}, u32[]{:S(2)}) collective-permute-start(bf16[1,192,1536]{2,1,0:T(8,128)(2,1)S(1)} %copy-done.3), channel_id=1, source_target_pairs={{0,2},{1,3},{2,0},{3,1},{4,6},{5,7},{6,4},{7,5}} | collective-permute-start | bytes 1769480 | tf_op jit(solution)/shard_map/ppermute | solution.py:703
  457.7 38.8 %collective-permute-start.25 = (bf16[1,384,768]{2,1,0:T(8,128)(2,1)}, bf16[1,384,768]{2,1,0:T(8,128)(2,1)S(1)}, u32[]{:S(2)}, u32[]{:S(2)}) collective-permute-start(bf16[1,384,768]{2,1,0:T(8,128)(2,1)} %collective-permute-done.24), channel_id=1, source_target_pairs={{0,1},{1,0},{2,3},{3,2},{4,5},{5,4},{6,7},{7,6}} | collective-permute-start | bytes 1769480 | tf_op jit(solution)/shard_map/ppermute | solution.py:710
  459.7 35.9 %collective-permute-start.28 = (bf16[1,192,768]{2,1,0:T(8,128)(2,1)S(1)}, bf16[1,192,768]{2,1,0:T(8,128)(2,1)S(1)}, u32[]{:S(2)}, u32[]{:S(2)}) collective-permute-start(bf16[1,192,768]{2,1,0:T(8,128)(2,1)S(1)} %copy-done.17), channel_id=1, source_target_pairs={{0,2},{1,3},{2,0},{3,1},{4,6},{5,7},{6,4},{7,5}} | collective-permute-start | bytes 884744 | tf_op jit(solution)/shard_map/ppermute | solution.py:703
  495.5 3.5 collective-permute-start.27
  495.5 9.2 %collective-permute-start.29 = (bf16[1,192,768]{2,1,0:T(8,128)(2,1)S(1)}, bf16[1,192,768]{2,1,0:T(8,128)(2,1)S(1)}, u32[]{:S(2)}, u32[]{:S(2)}) collective-permute-start(bf16[1,192,768]{2,1,0:T(8,128)(2,1)S(1)} %collective-permute-done.28), channel_id=1, source_target_pairs={{0,1},{1,0},{2,3},{3,2},{4,5},{5,4},{6,7},{7,6}} | collective-permute-start | bytes 884744 | tf_op jit(solution)/shard_map/ppermute | solution.py:710
  496.1 3.7 collective-permute-start.15
  496.1 5.4 %collective-permute-start.17 = (bf16[1,192,1536]{2,1,0:T(8,128)(2,1)S(1)}, bf16[1,192,1536]{2,1,0:T(8,128)(2,1)S(1)}, u32[]{:S(2)}, u32[]{:S(2)}) collective-permute-start(bf16[1,192,1536]{2,1,0:T(8,128)(2,1)S(1)} %collective-permute-done.16), channel_id=1, source_target_pairs={{0,1},{1,0},{2,3},{3,2},{4,5},{5,4},{6,7},{7,6}} | collective-permute-start | bytes 1769480 | tf_op jit(solution)/shard_map/ppermute | solution.py:710
  496.6 7.4 %collective-permute-start.19 = (bf16[1,192,1536]{2,1,0:T(8,128)(2,1)S(1)}, bf16[1,192,1536]{2,1,0:T(8,128)(2,1)S(1)}, u32[]{:S(2)}, u32[]{:S(2)}) collective-permute-start(bf16[1,192,1536]{2,1,0:T(8,128)(2,1)S(1)} %collective-permute-done.18), channel_id=1, source_target_pairs={{0,1},{1,0},{2,3},{3,2},{4,5},{5,4},{6,7},{7,6}} | collective-permute-start | bytes 1769480 | tf_op jit(solution)/shard_map/ppermute | solution.py:710
  (33 other events, 203.8 us)

commit v4 on v3

--- a/solution.py
+++ b/solution.py
@@ -311,7 +311,7 @@
     n_note, early_note = len(KINDS), len(KINDS) + 1
 
     def rows_of(index):
-        return pl.ds(0, TILE[0] if index in (n_note, early_note) else 1)
+        return pl.ds(0, PAIR if index == early_note else 1)
 
     def send_note(index):
         for slot, peer in enumerate(peers):
@@ -328,7 +328,7 @@
         rows, sem = pl.ds(first_row, end_row - first_row), len(KINDS) + PAIR + part
         return remote((held, mean)[part].at[AHEAD, rows], ahead.at[part, rows], note_sem.at[0, sem], note_sem.at[1, sem], FAR)
 
-    note[n_note] = n_sum[...]
+    note[n_note, :1, :] = jnp.sum(n_sum[...], axis=0, keepdims=True)
 
     def settle(group, _):
         grad_copies(group).wait_send()
@@ -343,7 +343,7 @@
         return 0
 
     lax.fori_loop(GROUPS - SEND_SLOTS, GROUPS, settle_means, 0)
-    total_sq = jnp.sum(jnp.sum(read_note(n_note), axis=0, keepdims=True), axis=1, keepdims=True)
+    total_sq = jnp.sum(read_note(n_note)[:1, :], axis=1, keepdims=True)
     clip = jnp.minimum(1.0, MAX_NORM / jnp.sqrt(total_sq))
     scal[len(KINDS)] = jnp.broadcast_to(clip, TILE)
 
@@ -376,7 +376,7 @@
         return [jnp.sum(sums[LAYERS * kind + layer], axis=0, keepdims=True) for sums in (u_sums, w_sums) for layer in range(layers)]
 
     def write_early_note():
-        for row, total in zip((0, LAYERS), tensor_sums(PROJ, 1)):
+        for row, total in enumerate(tensor_sums(PROJ, 1)):
             note[early_note, row:row + 1, :] = total
 
     def write_note(kind):
@@ -387,8 +387,8 @@
         note[kind, :1, :] = packed
 
     def early_ratio():
-        norms = jnp.sqrt(jnp.sum(read_note(early_note), axis=1, keepdims=True))
-        scal[PROJ, :1, :] = jnp.broadcast_to(norms[LAYERS:LAYERS + 1] / norms[:1], (1, TILE[1]))
+        norms = jnp.sqrt(jnp.sum(read_note(early_note)[:PAIR, :], axis=1, keepdims=True))
+        scal[PROJ, :1, :] = jnp.broadcast_to(norms[1:PAIR] / norms[:1], (1, TILE[1]))
 
     def ratios(kind):
         norms = jnp.sqrt(read_note(kind)[:1, :])

time: 507 us -> 506 us (level)
  no operation moved by 1% of the time
where the time goes in v4:
time: 506 us; the launch traced here: 505 us
  Pallas kernels  364 us (72%)
  local copies, waits for them, and re-layouts  41.9 us (8%)
  other arithmetic  38.6 us (8%)
  waiting for transfers between devices  37 us (7%)
  starting transfers between devices  22.8 us (5%)
    pallas_call x1, Pallas kernels, device_step(): pl.pallas_call(step_kernel, out_shape=out_shape, in_specs=[any_spec] * le...  353 us
    ppermute x9, waiting for transfers between devices, device_step(): far.append(lax.ppermute(piece, 'data', across))  37 us
    sub x4, other arithmetic, device_step(): state[kind] = (weight - LEARN_RATE * ratio * update, new_first, new_second)  36.5 us
    dynamic_update_slice x18, local copies, waits for them, and re-layouts, device_step(): lax.dynamic_update_slice(replicas[kind], piece, (layer, owners[k] * SHARD...  21.3 us
    unnamed x70, local copies, waits for them, and re-layouts  19.4 us
    pallas_call x1, Pallas kernels, assemble(): pl.pallas_call(assemble_kernel, out_shape=[shape(s, BF16) for s in whole]...  10.4 us
  transfers between devices with their start and end apart: 30, of which 2 were waited for; matrix products, arithmetic and copies ran while one was open for 12% of the time, Pallas kernels for 2%

profile of v4, /device:TPU:0, one launch (start us, length us, event | category | flops | bytes accessed | tf_op | source)
XLA Modules:
  0.0 505.0 jit_solution(1880616712340838538)
XLA Ops:
  0.6 353.4 %shard_map.279 = (f32[4,96,768]{2,1,0:T(8,128)}, f32[4,192,1152]{2,1,0:T(8,128)}, f32[4,192,1536]{2,1,0:T(8,128)}, f32[4,384,768]{2,1,0:T(8,128)}, bf16[4,384,76...) custom-call(f32[1,4,384,768]{3,2,1,0:T(8,128)} %refs_0_.1, ...), custom_call_target="tpu_custom_call" | custom-call | tf_op jit(solution)/shard_map/pallas_call | solution.py:669
  354.1 7.2 %collective-permute-start.10 = (bf16[1,192,768]{2,1,0:T(8,128)(2,1)}, bf16[1,192,768]{2,1,0:T(8,128)(2,1)S(1)}, u32[]{:S(2)}, u32[]{:S(2)}) collective-permute-start(bf16[1,192,768]{2,1,0:T(8,128)(2,1)} %get-tuple-element.51.refs_13_), channel_id=1, source_target_pairs={{0,1},{1,0},{2,3},{3,2},{4,5},{5,4},{6,7},{7,6}} | collective-permute-start | bytes 884744 | tf_op jit(solution)/shard_map/ppermute | solution.py:707
  361.3 2.7 collective-permute-start
  364.6 1.2 slice.16
  367.9 14.0 %multiply_subtract_fusion.1 = (f32[4,192,1536]{2,1,0:T(8,128)}, f32[4,192,1536]{2,1,0:T(8,128)}, f32[4,192,1536]{2,1,0:T(8,128)}) fusion(f32[4,192,1536]{2,1,0:T(8,128)} %refs_6_.1, f32[4]{0:T(128)S(1)} %get-tuple-element.63, f32[4,192,1536]{2,1,0:T(8,128)} %get-tuple-element.60, f32[]{:T(128)} %bitcast, f32[4,192,1536]{2,1,0:T(8,128)} %refs_10_.1, ...), kind=kLoop, calls=%fused_computation.7 | loop fusion | flops 18874368 | bytes 33030164 | tf_op jit(solution)/shard_map/sub | solution.py:700
  382.6 1.4 collective-permute-start.20
  384.8 5.6 %multiply_subtract_fusion.2 = (f32[4,192,1152]{2,1,0:T(8,128)}, f32[4,192,1152]{2,1,0:T(8,128)}, f32[4,192,1152]{2,1,0:T(8,128)}) fusion(f32[4,192,1152]{2,1,0:T(8,128)S(1)} %copy-done.26, f32[4]{0:T(128)S(1)} %get-tuple-element.65, f32[4,192,1152]{2,1,0:T(8,128)S(1)} %copy-done.32, f32[]{:T(128)} %bitcast, f32[4,192,1152]{2,1,0:T(8,128)S(1)} %copy-done.27, ...), kind=kLoop, calls=%fused_computation.10 | loop fusion | flops 14155776 | bytes 24772628 | tf_op jit(solution)/shard_map/sub | solution.py:700
  390.4 1.2 broadcast_select_fusion.refs_3_
  392.5 1.2 collective-permute-start.12
  394.5 4.4 collective-permute-done.20
  399.4 14.0 %multiply_subtract_fusion = (f32[4,384,768]{2,1,0:T(8,128)}, f32[4,384,768]{2,1,0:T(8,128)}, f32[4,384,768]{2,1,0:T(8,128)}) fusion(f32[4,384,768]{2,1,0:T(8,128)} %refs_7_.1, f32[4]{0:T(128)S(1)} %get-tuple-element.62, f32[4,384,768]{2,1,0:T(8,128)} %get-tuple-element.61, f32[]{:T(128)} %bitcast, f32[4,384,768]{2,1,0:T(8,128)} %refs_11_.1, ...), kind=kLoop, calls=%fused_computation.5 | loop fusion | flops 18874368 | bytes 33030164 | tf_op jit(solution)/shard_map/sub | solution.py:700
  414.2 1.4 collective-permute-start.24
  415.7 3.0 multiply_subtract_fusion.3
  419.3 3.0 copy-done
  422.3 1.1 copy-done.3
  423.4 1.1 copy-done.5
  424.5 1.1 copy-done.6
  425.5 1.1 copy-done.8
  426.6 1.1 copy-done.10
  427.7 1.1 copy-done.12
  428.7 1.1 copy-done.14
  429.8 1.1 copy-done.16
  435.7 10.4 %shard_map.280 = (bf16[4,384,768]{2,1,0:T(8,128)(2,1)}, bf16[4,768,1152]{2,1,0:T(8,128)(2,1)}, bf16[4,768,1536]{2,1,0:T(8,128)(2,1)}, bf16[4,1536,768]{2,1,0:T(8,128)(2,1)}) custom-call(bf16[4,384,768]{2,1,0:T(8,128)(2,1)S(1)} %copy-done.1, bf16[4,768,1152]{2,1,0:T(8,128)(2,1)S(1)} %copy-done, bf16[4,96,384]{2,1,0:T(8,128)(2,1)S(1)} %copy-done.19, ...), custom_call_target="tpu_custom_call" | custom-call | flops 12000000 | bytes 38000000 | tf_op jit(solution)/shard_map/pallas_call | solution.py:629
  446.1 1.9 constant_dynamic-update-slice_fusion.9
  448.0 1.4 collective-permute-start.14
  449.5 1.9 constant_dynamic-update-slice_fusion.8
  451.4 1.9 constant_dynamic-update-slice_fusion.7
  453.9 1.9 constant_dynamic-update-slice_fusion.6
  455.8 1.4 collective-permute-start.18
  457.2 1.9 constant_dynamic-update-slice_fusion.17
  459.8 1.9 constant_dynamic-update-slice_fusion.5
  462.5 32.5 %collective-permute-done.28 = bf16[1,192,768]{2,1,0:T(8,128)(2,1)S(1)} collective-permute-done((bf16[1,192,768]{2,1,0:T(8,128)(2,1)S(1)}, bf16[1,192,768]{2,1,0:T(8,128)(2,1)S(1)}, u32[]{:S(2)}, u32[]{:S(2)}) %collective-permute-start.28) | collective-permute-done | bytes 294944 | tf_op jit(solution)/shard_map/ppermute | solution.py:703
  (125 shorter events, 24.6 us)
Async XLA Ops:
  354.1 12.5 %collective-permute-start.10 = (bf16[1,192,768]{2,1,0:T(8,128)(2,1)}, bf16[1,192,768]{2,1,0:T(8,128)(2,1)S(1)}, u32[]{:S(2)}, u32[]{:S(2)}) collective-permute-start(bf16[1,192,768]{2,1,0:T(8,128)(2,1)} %get-tuple-element.51.refs_13_), channel_id=1, source_target_pairs={{0,1},{1,0},{2,3},{3,2},{4,5},{5,4},{6,7},{7,6}} | collective-permute-start | bytes 884744 | tf_op jit(solution)/shard_map/ppermute | solution.py:707
  361.3 23.3 %collective-permute-start = (bf16[10,96,384]{2,1,0:T(8,128)(2,1)}, bf16[10,96,384]{2,1,0:T(8,128)(2,1)S(1)}, u32[]{:S(2)}, u32[]{:S(2)}) collective-permute-start(bf16[10,96,384]{2,1,0:T(8,128)(2,1)} %get-tuple-element.42), channel_id=1, source_target_pairs={{0,2},{2,0},{4,6},{6,4}} | collective-permute-start | bytes 2211848 | tf_op jit(solution)/shard_map/ppermute | solution.py:704
  364.0 20.0 %collective-permute-start.3 = (bf16[1,192,1536]{2,1,0:T(8,128)(2,1)}, bf16[1,192,1536]{2,1,0:T(8,128)(2,1)S(1)}, u32[]{:S(2)}, u32[]{:S(2)}) collective-permute-start(bf16[1,192,1536]{2,1,0:T(8,128)(2,1)} %get-tuple-element.44.refs_6_), channel_id=1, source_target_pairs={{0,1},{1,0},{2,3},{3,2},{4,5},{5,4},{6,7},{7,6}} | collective-permute-start | bytes 1769480 | tf_op jit(solution)/shard_map/ppermute | solution.py:707
  364.0 20.2 %collective-permute-start.4 = (bf16[1,192,1536]{2,1,0:T(8,128)(2,1)}, bf16[1,192,1536]{2,1,0:T(8,128)(2,1)S(1)}, u32[]{:S(2)}, u32[]{:S(2)}) collective-permute-start(bf16[1,192,1536]{2,1,0:T(8,128)(2,1)} %get-tuple-element.45.refs_7_), channel_id=1, source_target_pairs={{0,1},{1,0},{2,3},{3,2},{4,5},{5,4},{6,7},{7,6}} | collective-permute-start | bytes 1769480 | tf_op jit(solution)/shard_map/ppermute | solution.py:707
  364.5 17.3 %collective-permute-start.11 = (bf16[1,192,768]{2,1,0:T(8,128)(2,1)}, bf16[1,192,768]{2,1,0:T(8,128)(2,1)S(1)}, u32[]{:S(2)}, u32[]{:S(2)}) collective-permute-start(bf16[1,192,768]{2,1,0:T(8,128)(2,1)} %get-tuple-element.52.refs_14_), channel_id=1, source_target_pairs={{0,1},{1,0},{2,3},{3,2},{4,5},{5,4},{6,7},{7,6}} | collective-permute-start | bytes 884744 | tf_op jit(solution)/shard_map/ppermute | solution.py:707
  367.3 15.2 %collective-permute-start.1 = (bf16[4,96,384]{2,1,0:T(8,128)(2,1)}, bf16[4,96,384]{2,1,0:T(8,128)(2,1)S(1)}, u32[]{:S(2)}, u32[]{:S(2)}) collective-permute-start(bf16[4,96,384]{2,1,0:T(8,128)(2,1)} %get-tuple-element.41.refs_2_), channel_id=1, source_target_pairs={{0,1},{1,0},{2,3},{3,2},{4,5},{5,4},{6,7},{7,6}} | collective-permute-start | bytes 884744 | tf_op jit(solution)/shard_map/ppermute | solution.py:706
  367.8 16.9 %copy-start.26 = (f32[4,192,1152]{2,1,0:T(8,128)S(1)}, f32[4,192,1152]{2,1,0:T(8,128)}, u32[]{:S(2)}) copy-start(f32[4,192,1152]{2,1,0:T(8,128)} %refs_5_.1) | copy-start | bytes 10616836
  367.8 16.9 %copy-start.27 = (f32[4,192,1152]{2,1,0:T(8,128)S(1)}, f32[4,192,1152]{2,1,0:T(8,128)}, u32[]{:S(2)}) copy-start(f32[4,192,1152]{2,1,0:T(8,128)} %refs_9_.1) | copy-start | bytes 10616836
  382.5 11.1 %collective-permute-start.7 = (bf16[1,384,768]{2,1,0:T(8,128)(2,1)S(1)}, bf16[1,384,768]{2,1,0:T(8,128)(2,1)S(1)}, u32[]{:S(2)}, u32[]{:S(2)}) collective-permute-start(bf16[1,384,768]{2,1,0:T(8,128)(2,1)S(1)} %copy-done.7), channel_id=1, source_target_pairs={{0,1},{1,0},{2,3},{3,2},{4,5},{5,4},{6,7},{7,6}} | collective-permute-start | bytes 1769480 | tf_op jit(solution)/shard_map/ppermute | solution.py:707
  382.6 16.3 %collective-permute-start.20 = (bf16[1,384,768]{2,1,0:T(8,128)(2,1)S(1)}, bf16[1,384,768]{2,1,0:T(8,128)(2,1)}, u32[]{:S(2)}, u32[]{:S(2)}) collective-permute-start(bf16[1,384,768]{2,1,0:T(8,128)(2,1)S(1)} %copy-done.7), channel_id=1, source_target_pairs={{0,2},{1,3},{2,0},{3,1},{4,6},{5,7},{6,4},{7,5}} | collective-permute-start | bytes 1769480 | tf_op jit(solution)/shard_map/ppermute | solution.py:703
  384.0 7.6 %collective-permute-start.5 = (bf16[1,192,1536]{2,1,0:T(8,128)(2,1)S(1)}, bf16[1,192,1536]{2,1,0:T(8,128)(2,1)}, u32[]{:S(2)}, u32[]{:S(2)}) collective-permute-start(bf16[1,192,1536]{2,1,0:T(8,128)(2,1)S(1)} %copy-done.4), channel_id=1, source_target_pairs={{0,1},{1,0},{2,3},{3,2},{4,5},{5,4},{6,7},{7,6}} | collective-permute-start | bytes 1769480 | tf_op jit(solution)/shard_map/ppermute | solution.py:707
  384.2 8.3 %collective-permute-start.6 = (bf16[1,192,1536]{2,1,0:T(8,128)(2,1)S(1)}, bf16[1,192,1536]{2,1,0:T(8,128)(2,1)}, u32[]{:S(2)}, u32[]{:S(2)}) collective-permute-start(bf16[1,192,1536]{2,1,0:T(8,128)(2,1)S(1)} %copy-done.2), channel_id=1, source_target_pairs={{0,1},{1,0},{2,3},{3,2},{4,5},{5,4},{6,7},{7,6}} | collective-permute-start | bytes 1769480 | tf_op jit(solution)/shard_map/ppermute | solution.py:707
  384.6 14.3 %collective-permute-start.8 = (bf16[1,384,768]{2,1,0:T(8,128)(2,1)}, bf16[1,384,768]{2,1,0:T(8,128)(2,1)}, u32[]{:S(2)}, u32[]{:S(2)}) collective-permute-start(bf16[1,384,768]{2,1,0:T(8,128)(2,1)} %get-tuple-element.49.refs_11_), channel_id=1, source_target_pairs={{0,1},{1,0},{2,3},{3,2},{4,5},{5,4},{6,7},{7,6}} | collective-permute-start | bytes 1769480 | tf_op jit(solution)/shard_map/ppermute | solution.py:707
  391.6 24.1 %collective-permute-start.22 = (bf16[1,384,768]{2,1,0:T(8,128)(2,1)}, bf16[1,384,768]{2,1,0:T(8,128)(2,1)}, u32[]{:S(2)}, u32[]{:S(2)}) collective-permute-start(bf16[1,384,768]{2,1,0:T(8,128)(2,1)} %get-tuple-element.49.refs_11_), channel_id=1, source_target_pairs={{0,2},{1,3},{2,0},{3,1},{4,6},{5,7},{6,4},{7,5}} | collective-permute-start | bytes 1769480 | tf_op jit(solution)/shard_map/ppermute | solution.py:703
  392.5 55.5 %collective-permute-start.12 = (bf16[1,192,1536]{2,1,0:T(8,128)(2,1)}, bf16[1,192,1536]{2,1,0:T(8,128)(2,1)}, u32[]{:S(2)}, u32[]{:S(2)}) collective-permute-start(bf16[1,192,1536]{2,1,0:T(8,128)(2,1)} %get-tuple-element.44.refs_6_), channel_id=1, source_target_pairs={{0,2},{1,3},{2,0},{3,1},{4,6},{5,7},{6,4},{7,5}} | collective-permute-start | bytes 1769480 | tf_op jit(solution)/shard_map/ppermute | solution.py:703
  394.5 19.0 %collective-permute-start.9 = (bf16[1,384,768]{2,1,0:T(8,128)(2,1)}, bf16[1,384,768]{2,1,0:T(8,128)(2,1)S(1)}, u32[]{:S(2)}, u32[]{:S(2)}) collective-permute-start(bf16[1,384,768]{2,1,0:T(8,128)(2,1)} %get-tuple-element.50.refs_12_), channel_id=1, source_target_pairs={{0,1},{1,0},{2,3},{3,2},{4,5},{5,4},{6,7},{7,6}} | collective-permute-start | bytes 1769480 | tf_op jit(solution)/shard_map/ppermute | solution.py:707
  398.9 50.6 %collective-permute-start.21 = (bf16[1,384,768]{2,1,0:T(8,128)(2,1)}, bf16[1,384,768]{2,1,0:T(8,128)(2,1)}, u32[]{:S(2)}, u32[]{:S(2)}) collective-permute-start(bf16[1,384,768]{2,1,0:T(8,128)(2,1)} %collective-permute-done.20), channel_id=1, source_target_pairs={{0,1},{1,0},{2,3},{3,2},{4,5},{5,4},{6,7},{7,6}} | collective-permute-start | bytes 1769480 | tf_op jit(solution)/shard_map/ppermute | solution.py:710
  398.9 19.8 %collective-permute-start.2 = (bf16[10,96,384]{2,1,0:T(8,128)(2,1)S(1)}, bf16[10,96,384]{2,1,0:T(8,128)(2,1)}, u32[]{:S(2)}, u32[]{:S(2)}) collective-permute-start(bf16[10,96,384]{2,1,0:T(8,128)(2,1)S(1)} %broadcast_select_fusion.refs_3_), channel_id=1, source_target_pairs={{0,1},{1,0},{2,3},{3,2},{4,5},{5,4},{6,7},{7,6}} | collective-permute-start | bytes 2211848 | tf_op jit(solution)/shard_map/ppermute | solution.py:706
  414.2 43.0 %collective-permute-start.24 = (bf16[1,384,768]{2,1,0:T(8,128)(2,1)}, bf16[1,384,768]{2,1,0:T(8,128)(2,1)}, u32[]{:S(2)}, u32[]{:S(2)}) collective-permute-start(bf16[1,384,768]{2,1,0:T(8,128)(2,1)} %get-tuple-element.50.refs_12_), channel_id=1, source_target_pairs={{0,2},{1,3},{2,0},{3,1},{4,6},{5,7},{6,4},{7,5}} | collective-permute-start | bytes 1769480 | tf_op jit(solution)/shard_map/ppermute | solution.py:703
  415.7 37.6 %collective-permute-start.23 = (bf16[1,384,768]{2,1,0:T(8,128)(2,1)}, bf16[1,384,768]{2,1,0:T(8,128)(2,1)}, u32[]{:S(2)}, u32[]{:S(2)}) collective-permute-start(bf16[1,384,768]{2,1,0:T(8,128)(2,1)} %collective-permute-done.22), channel_id=1, source_target_pairs={{0,1},{1,0},{2,3},{3,2},{4,5},{5,4},{6,7},{7,6}} | collective-permute-start | bytes 1769480 | tf_op jit(solution)/shard_map/ppermute | solution.py:710
  418.7 37.1 %collective-permute-start.26 = (bf16[1,192,768]{2,1,0:T(8,128)(2,1)}, bf16[1,192,768]{2,1,0:T(8,128)(2,1)S(1)}, u32[]{:S(2)}, u32[]{:S(2)}) collective-permute-start(bf16[1,192,768]{2,1,0:T(8,128)(2,1)} %get-tuple-element.51.refs_13_), channel_id=1, source_target_pairs={{0,2},{1,3},{2,0},{3,1},{4,6},{5,7},{6,4},{7,5}} | collective-permute-start | bytes 884744 | tf_op jit(solution)/shard_map/ppermute | solution.py:703
  448.0 47.0 %collective-permute-start.14 = (bf16[1,192,1536]{2,1,0:T(8,128)(2,1)S(1)}, bf16[1,192,1536]{2,1,0:T(8,128)(2,1)S(1)}, u32[]{:S(2)}, u32[]{:S(2)}) collective-permute-start(bf16[1,192,1536]{2,1,0:T(8,128)(2,1)S(1)} %copy-done.6), channel_id=1, source_target_pairs={{0,2},{1,3},{2,0},{3,1},{4,6},{5,7},{6,4},{7,5}} | collective-permute-start | bytes 1769480 | tf_op jit(solution)/shard_map/ppermute | solution.py:703
  449.4 9.7 %collective-permute-start.13 = (bf16[1,192,1536]{2,1,0:T(8,128)(2,1)}, bf16[1,192,1536]{2,1,0:T(8,128)(2,1)S(1)}, u32[]{:S(2)}, u32[]{:S(2)}) collective-permute-start(bf16[1,192,1536]{2,1,0:T(8,128)(2,1)} %collective-permute-done.12), channel_id=1, source_target_pairs={{0,1},{1,0},{2,3},{3,2},{4,5},{5,4},{6,7},{7,6}} | collective-permute-start | bytes 1769480 | tf_op jit(solution)/shard_map/ppermute | solution.py:710
  453.3 42.3 %collective-permute-start.16 = (bf16[1,192,1536]{2,1,0:T(8,128)(2,1)S(1)}, bf16[1,192,1536]{2,1,0:T(8,128)(2,1)S(1)}, u32[]{:S(2)}, u32[]{:S(2)}) collective-permute-start(bf16[1,192,1536]{2,1,0:T(8,128)(2,1)S(1)} %copy-done.5), channel_id=1, source_target_pairs={{0,2},{1,3},{2,0},{3,1},{4,6},{5,7},{6,4},{7,5}} | collective-permute-start | bytes 1769480 | tf_op jit(solution)/shard_map/ppermute | solution.py:703
  455.8 39.8 %collective-permute-start.18 = (bf16[1,192,1536]{2,1,0:T(8,128)(2,1)S(1)}, bf16[1,192,1536]{2,1,0:T(8,128)(2,1)S(1)}, u32[]{:S(2)}, u32[]{:S(2)}) collective-permute-start(bf16[1,192,1536]{2,1,0:T(8,128)(2,1)S(1)} %copy-done.3), channel_id=1, source_target_pairs={{0,2},{1,3},{2,0},{3,1},{4,6},{5,7},{6,4},{7,5}} | collective-permute-start | bytes 1769480 | tf_op jit(solution)/shard_map/ppermute | solution.py:703
  457.2 38.9 %collective-permute-start.25 = (bf16[1,384,768]{2,1,0:T(8,128)(2,1)}, bf16[1,384,768]{2,1,0:T(8,128)(2,1)S(1)}, u32[]{:S(2)}, u32[]{:S(2)}) collective-permute-start(bf16[1,384,768]{2,1,0:T(8,128)(2,1)} %collective-permute-done.24), channel_id=1, source_target_pairs={{0,1},{1,0},{2,3},{3,2},{4,5},{5,4},{6,7},{7,6}} | collective-permute-start | bytes 1769480 | tf_op jit(solution)/shard_map/ppermute | solution.py:710
  459.2 35.9 %collective-permute-start.28 = (bf16[1,192,768]{2,1,0:T(8,128)(2,1)S(1)}, bf16[1,192,768]{2,1,0:T(8,128)(2,1)S(1)}, u32[]{:S(2)}, u32[]{:S(2)}) collective-permute-start(bf16[1,192,768]{2,1,0:T(8,128)(2,1)S(1)} %copy-done.17), channel_id=1, source_target_pairs={{0,2},{1,3},{2,0},{3,1},{4,6},{5,7},{6,4},{7,5}} | collective-permute-start | bytes 884744 | tf_op jit(solution)/shard_map/ppermute | solution.py:703
  495.1 3.5 collective-permute-start.27
  495.1 9.2 %collective-permute-start.29 = (bf16[1,192,768]{2,1,0:T(8,128)(2,1)S(1)}, bf16[1,192,768]{2,1,0:T(8,128)(2,1)S(1)}, u32[]{:S(2)}, u32[]{:S(2)}) collective-permute-start(bf16[1,192,768]{2,1,0:T(8,128)(2,1)S(1)} %collective-permute-done.28), channel_id=1, source_target_pairs={{0,1},{1,0},{2,3},{3,2},{4,5},{5,4},{6,7},{7,6}} | collective-permute-start | bytes 884744 | tf_op jit(solution)/shard_map/ppermute | solution.py:710
  495.6 3.7 collective-permute-start.15
  495.6 5.4 %collective-permute-start.17 = (bf16[1,192,1536]{2,1,0:T(8,128)(2,1)S(1)}, bf16[1,192,1536]{2,1,0:T(8,128)(2,1)S(1)}, u32[]{:S(2)}, u32[]{:S(2)}) collective-permute-start(bf16[1,192,1536]{2,1,0:T(8,128)(2,1)S(1)} %collective-permute-done.16), channel_id=1, source_target_pairs={{0,1},{1,0},{2,3},{3,2},{4,5},{5,4},{6,7},{7,6}} | collective-permute-start | bytes 1769480 | tf_op jit(solution)/shard_map/ppermute | solution.py:710
  496.1 7.4 %collective-permute-start.19 = (bf16[1,192,1536]{2,1,0:T(8,128)(2,1)S(1)}, bf16[1,192,1536]{2,1,0:T(8,128)(2,1)S(1)}, u32[]{:S(2)}, u32[]{:S(2)}) collective-permute-start(bf16[1,192,1536]{2,1,0:T(8,128)(2,1)S(1)} %collective-permute-done.18), channel_id=1, source_target_pairs={{0,1},{1,0},{2,3},{3,2},{4,5},{5,4},{6,7},{7,6}} | collective-permute-start | bytes 1769480 | tf_op jit(solution)/shard_map/ppermute | solution.py:710
  (33 other events, 203.6 us)
